TPU v7x, 32 devices: a whole 2x2x4 slice. The times are simulated.
32 devices in a mesh: gy: 8 (over y, x, core), gx: 4 (over z).
Axes of the slice: x: 2, y: 2, z: 4, core: 2. Of those that a mesh axis runs over, the one named last changes fastest.
Arguments:
- position: float32 [16, 32, 128, 3], P('gy', 'gx'), may hold values from 0 to 1
- velocity: float32 [16, 32, 128, 3], P('gy', 'gx'), may hold values from -6 to 6
- particle_mass: float32 [16, 32, 128], P('gy', 'gx'), may hold values from 0.006 to 0.025
- cell_counts: int32 [16, 32], P('gy', 'gx'), may hold values from 64 to 128
- shear_shift: int32 [1], replicated, may hold values from 12 to 20
Outputs:
- density: float32 [16, 32, 128], P('gy', 'gx')
- acceleration: float32 [16, 32, 128, 3], P('gy', 'gx')
Inputs may be any that keep to these rules, and one draw needn't show every extreme that they name: `shear_shift`: the offset is a whole number of cells from 12 to 20.
All inputs are finite; a program needn't handle non-finite values.
Results may differ from a plain program's by a relative error of at most 0.0003.
Values sent between devices are 32-bit elements; how exact they have to be, the bound alone decides.
A program may use at most 64 MiB of HBM per device.

v0:
```python
import functools
import math

import jax
import jax.numpy as jnp
from jax import lax
from jax.experimental import pallas as pl
from jax.experimental.pallas import tpu as pltpu
from jax.sharding import PartitionSpec as P

SMOOTHING = 0.5
KERNEL_NORM = 1.0 / (math.pi * SMOOTHING**3)
SOUND_SQ = 0.2
VISCOSITY = 0.05
SOFTENING = 0.0025
SHEAR_JUMP = 1.0

MESH = pl.DeviceIdType.MESH
W_SCALE = 0.25 * KERNEL_NORM
G_SCALE = -0.75 * KERNEL_NORM / (SMOOTHING * SMOOTHING)
SOFT_Q = SOFTENING / (SMOOTHING * SMOOTHING)
TINY = 1e-10
FEATURES = 48


def split3(p):
    h = p.astype(jnp.bfloat16).astype(jnp.float32)
    rest = p - h
    m = rest.astype(jnp.bfloat16).astype(jnp.float32)
    return h, m, rest - m


def split2(p):
    h = p.astype(jnp.bfloat16).astype(jnp.float32)
    return jnp.concatenate([h, p - h], axis=0).astype(jnp.bfloat16)


def dot(a, b):
    return jnp.dot(a, b, preferred_element_type=jnp.float32)


def kernel(
    n, m, pos_ref, vel_ref, mass_ref, counts_ref, shift_ref, dens_ref, acc_ref,
    own, above, below, left, right, pad,
    rho, rho_above, rho_below, rho_left, rho_right, rho_pad,
    feat, mass_wide, moments, flows, wides, partial, g_pairs, l_pairs,
    send_sem, recv_sem, rho_send_sem, rho_recv_sem,
):
    rows, _, cols, slots = pos_ref.shape
    gy, gx = lax.axis_index("gy"), lax.axis_index("gx")
    half, reach = n // 2, cols // 2
    at_top, at_bottom = gy == m - 1, gy == 0
    up, down = lax.rem(gy + 1, m), lax.rem(gy + m - 1, m)
    off_up = jnp.where(at_top, half, 0)
    off_down = jnp.where(at_bottom, half, 0)

    def beside(off, k):
        return lax.rem(gx + 2 * n - off - k, n)

    partners = [(up, beside(off_up, k)) for k in (-1, 0, 1)]
    partners += [(down, beside(off_down, k)) for k in (-1, 0, 1)]
    partners += [(gy, beside(0, k)) for k in (-1, 1)]

    def copy_to(src, dst, sends, recvs, i, device):
        return pltpu.make_async_remote_copy(
            src_ref=src, dst_ref=dst, send_sem=sends.at[i], recv_sem=recvs.at[i],
            device_id=device, device_id_type=MESH,
        )

    def rows_to(mine_row, ghost, sends, recvs, base, slab, off, full):
        copies = []
        for k in (-1, 0, 1):
            count = cols if k == 0 else reach + 1 if full else 1
            edge = cols - count if k == -1 else 0
            src = mine_row.at[pl.ds(edge, count)]
            dst = ghost.at[pl.ds((k + 1) * cols + edge, count)]
            copies.append(copy_to(src, dst, sends, recvs, base + k + 1, (slab, beside(off, k))))
        return copies

    def both_ways(wrapped, make, act):
        @pl.when(wrapped)
        def _():
            for copy in make(True):
                act(copy)

        @pl.when(jnp.logical_not(wrapped))
        def _():
            for copy in make(False):
                act(copy)

    def start(copy):
        copy.start()

    def sent(copy):
        copy.wait_send()

    def received(copy):
        copy.wait_recv()

    def to_up(mine, ghost, sends, recvs):
        return lambda full: rows_to(mine.at[rows - 1], ghost, sends, recvs, 0, up, off_up, full)

    def to_down(mine, ghost, sends, recvs):
        return lambda full: rows_to(mine.at[0], ghost, sends, recvs, 3, down, off_down, full)

    def to_sides(mine, from_left, from_right, sends, recvs):
        return [
            copy_to(mine.at[:, 0], from_right, sends, recvs, 6, (gy, beside(0, 1))),
            copy_to(mine.at[:, cols - 1], from_left, sends, recvs, 7, (gy, beside(0, -1))),
        ]

    barrier = pltpu.get_barrier_semaphore()
    for device in partners:
        pl.semaphore_signal(barrier, inc=1, device_id=device, device_id_type=MESH)

    lane = lax.broadcasted_iota(jnp.int32, (1, slots), 1)
    for r in range(rows):
        for c in range(cols):
            for k in range(3):
                own[r, c, pl.ds(k, 1), :] = pos_ref[r, k, pl.ds(c, 1), :]
                own[r, c, pl.ds(3 + k, 1), :] = vel_ref[r, k, pl.ds(c, 1), :]
            w = jnp.where(lane < counts_ref[r, c], mass_ref[r, pl.ds(c, 1), :], 0.0)
            own[r, c, pl.ds(6, 1), :] = w
            own[r, c, pl.ds(7, 1), :] = jnp.zeros_like(w)

    pl.semaphore_wait(barrier, len(partners))
    first_up = to_up(own, below, send_sem, recv_sem)
    first_down = to_down(own, above, send_sem, recv_sem)
    first_sides = to_sides(own, left, right, send_sem, recv_sem)
    both_ways(at_top, first_up, start)
    both_ways(at_bottom, first_down, start)
    for copy in first_sides:
        copy.start()

    shift = shift_ref[0]
    total_half = half * cols
    lag = jnp.clip(shift - total_half, -reach, reach)
    start_above = cols - 1 - jnp.where(at_top, lag, 0)
    start_below = cols - 1 + jnp.where(at_bottom, lag, 0)
    row8 = lax.broadcasted_iota(jnp.int32, (8, slots), 0)
    is_vx = jnp.where(row8 == 3, SHEAR_JUMP, 0.0)
    jump_above = jnp.where(at_top, 1.0, 0.0) * is_vx
    jump_below = jnp.where(at_bottom, 1.0, 0.0) * is_vx

    wide = cols + 2
    mass_row = jnp.where(row8 == 5, 1.0, 0.0)
    none = jnp.zeros_like(mass_row)
    mass_pick = jnp.concatenate([mass_row, none, mass_row, none, mass_row, none], axis=0)
    mass_pick = mass_pick.astype(jnp.bfloat16)

    def prepare(r, c, f):
        pad[r, c] = f
        x = jnp.where(row8 < 3, 2.0 * f - 1.0, 0.0)
        norm = jnp.sum(x * x, axis=0, keepdims=True)
        w = jnp.broadcast_to(f[6:7], f.shape)
        p = jnp.where(row8 == 3, norm, x)
        p = jnp.where(row8 == 4, 1.0, p)
        p = jnp.where(row8 == 5, w, p)
        h, mid, low = split3(p)
        stacked = jnp.concatenate([h, h, mid, h, low, mid], axis=0)
        turned = stacked.T.astype(jnp.bfloat16)
        feat[r, c] = turned
        mass_wide[r, c] = dot(turned, mass_pick)
        moment = jnp.where(row8 % 4 == 0, 1.0, f[2:3] - 0.5)
        moment = jnp.where(row8 % 4 == 1, f[0:1] - 0.5, moment)
        moment = jnp.where(row8 % 4 == 2, f[1:2] - 0.5, moment)
        moments[r, c] = moment * w
        flow = jnp.where(row8 == 0, 1.0, f[5:6])
        flow = jnp.where(row8 == 1, f[3:4], flow)
        flow = jnp.where(row8 == 2, f[4:5], flow)
        flows[r, c] = jnp.where(row8 < 4, flow, 0.0) * w
        wides[r, c] = w

    def prepare_row(r, carry):
        for c in range(cols):
            prepare(r + 1, c + 1, own[r, c])
        return carry

    lax.fori_loop(0, rows, prepare_row, 0)

    near = [(a, b) for a in (-1, 0, 1) for b in (-1, 0, 1)]

    def add_pairs(r, c, total, pairs):
        i = r * cols + c
        x = 2.0 * pad[r + 1, c + 1] - 1.0
        for a, b in pairs:
            offset = jnp.where(row8 == 0, 2.0 * b, jnp.where(row8 == 1, 2.0 * a, 0.0))
            u = jnp.where(row8 < 3, x - offset, 0.0)
            norm = jnp.sum(u * u, axis=0, keepdims=True)
            p = jnp.where(row8 == 3, 1.0, -2.0 * u)
            p = jnp.where(row8 == 4, norm, p)
            h, mid, low = split3(p)
            stacked = jnp.concatenate([h, mid, h, low, h, mid], axis=0).astype(jnp.bfloat16)
            s = dot(feat[r + 1 + a, c + 1 + b], stacked)
            s = jnp.maximum(s, TINY)
            inv = lax.rsqrt(s)
            q = s * inv
            outer = 2.0 - q
            inner = jnp.maximum(outer - q, 0.0)
            outer = jnp.maximum(outer, 0.0)
            inner_sq = inner * inner
            slope = outer * outer - inner_sq
            value = (outer * slope + inner_sq) * mass_wide[r + 1 + a, c + 1 + b]
            total = total + jnp.sum(value.reshape(slots // 8, 8, slots), axis=0)
            g = slope * inv
            index = near.index((a, b))
            g_high = g.astype(jnp.bfloat16)
            g_pairs[i, pl.ds(index * 2 * slots, slots), :] = g_high
            g_pairs[i, pl.ds(index * 2 * slots + slots, slots), :] = (
                g - g_high.astype(jnp.float32)
            ).astype(jnp.bfloat16)
            l_pairs[i, pl.ds(index * slots, slots), :] = (g * (1.0 / (s + SOFT_Q))).astype(
                jnp.bfloat16
            )
        return total

    zero8 = jnp.zeros((8, slots), jnp.float32)

    def finish(r, c, total):
        row = W_SCALE * jnp.sum(total, axis=0, keepdims=True)
        occupied = pad[r + 1, c + 1, 6:7] > 0.0
        dens_ref[r, pl.ds(c, 1), :] = jnp.where(occupied, row, 0.0)
        rho[r, c] = 1.0 / jnp.where(occupied, row, 1.0)

    def near_own(r):
        return [(a, b) for a, b in near if 0 <= r + a < rows]

    def near_ghost(r):
        return [(a, b) for a, b in near if not 0 <= r + a < rows]

    def density_own(r):
        def step(c, carry):
            partial[r, c] = add_pairs(r, c, zero8, near_own(r))
            return carry

        lax.fori_loop(1, cols - 1, step, 0, unroll=3)

    def density_ghost(r):
        def step(c, carry):
            finish(r, c, add_pairs(r, c, partial[r, c], near_ghost(r)))
            return carry

        lax.fori_loop(1, cols - 1, step, 0, unroll=3)

        def edge(k, carry):
            c = k * (cols - 1)
            finish(r, c, add_pairs(r, c, zero8, near))
            return carry

        lax.fori_loop(0, 2, edge, 0, unroll=2)

    for r in range(rows):
        density_own(r)

    both_ways(at_bottom, first_up, received)
    both_ways(at_top, first_down, received)
    for copy in first_sides:
        copy.wait_recv()
    for r in range(rows):
        prepare(r + 1, 0, left[r])
        prepare(r + 1, cols + 1, right[r])

    for t in range(wide):
        prepare(0, t, below[start_below + t] - jump_below)
    for t in range(wide):
        prepare(rows + 1, t, above[start_above + t] + jump_above)

    second_up = to_up(rho, rho_below, rho_send_sem, rho_recv_sem)
    second_down = to_down(rho, rho_above, rho_send_sem, rho_recv_sem)
    second_sides = to_sides(rho, rho_left, rho_right, rho_send_sem, rho_recv_sem)
    density_ghost(0)
    both_ways(at_bottom, second_down, start)
    for r in range(1, rows):
        density_ghost(r)
    both_ways(at_top, second_up, start)
    for copy in second_sides:
        copy.start()
    for r in range(rows):
        for c in range(cols):
            rho_pad[r + 1, c + 1] = rho[r, c]
    both_ways(at_top, second_down, received)
    for t in range(wide):
        rho_pad[rows + 1, t] = rho_above[start_above + t]

    upper_half = row8 >= 4

    def force(r, c):
        i = r * cols + c
        f = pad[r + 1, c + 1]
        mine = rho_pad[r + 1, c + 1]
        g_lhs, k_lhs = [], []
        for a, b in near:
            inverse = jnp.broadcast_to(rho_pad[r + 1 + a, c + 1 + b], f.shape)
            w = wides[r + 1 + a, c + 1 + b]
            moment = moments[r + 1 + a, c + 1 + b]
            offset = jnp.where(row8 % 4 == 1, float(b), jnp.where(row8 % 4 == 2, float(a), 0.0))
            moment = moment + offset * w
            g_rows = split2(jnp.where(upper_half, moment * inverse, moment))
            k_rows = split2(flows[r + 1 + a, c + 1 + b] * inverse)
            both = jnp.concatenate([g_rows, k_rows], axis=0)
            g_lhs += [both, both]
            k_lhs.append(k_rows)
        sums = dot(jnp.concatenate(g_lhs, axis=1), g_pairs[i])
        soft = dot(jnp.concatenate(k_lhs, axis=1), l_pairs[i])
        g_sum = sums[0:8] + sums[8:16]
        k_sum = (sums[16:24] + sums[24:32]) - SOFT_Q * (soft[0:8] + soft[8:16])
        here = f[0:3] - 0.5
        plain = here * g_sum[0:1] - g_sum[1:4]
        weighed = here * g_sum[4:5] - g_sum[5:8]
        pressure = -SOUND_SQ * (mine * plain + weighed)
        viscous = (2.0 * VISCOSITY) * mine * (f[3:6] * k_sum[0:1] - k_sum[1:4])
        accel = jnp.where(f[6:7] > 0.0, G_SCALE * (pressure + viscous), 0.0)
        for k in range(3):
            acc_ref[r, k, pl.ds(c, 1), :] = accel[k : k + 1]

    def force_inner(c, carry):
        force(rows - 1, 2 * c + 1)
        force(rows - 1, 2 * c + 2)
        return carry

    early = (cols - 2) // 2 if rows > 1 else 0
    lax.fori_loop(0, early, force_inner, 0)

    both_ways(at_bottom, second_up, received)
    for copy in second_sides:
        copy.wait_recv()
    for r in range(rows):
        rho_pad[r + 1, 0] = rho_left[r]
        rho_pad[r + 1, cols + 1] = rho_right[r]
    for t in range(wide):
        rho_pad[0, t] = rho_below[start_below + t]

    force(rows - 1, 0)
    for c in range(2 * early + 1, cols):
        force(rows - 1, c)

    def force_pair(i, carry):
        force(i // (cols // 2), 2 * (i % (cols // 2)))
        force(i // (cols // 2), 2 * (i % (cols // 2)) + 1)
        return carry

    lax.fori_loop(0, (rows - 1) * (cols // 2), force_pair, 0)
    both_ways(at_top, first_up, sent)
    both_ways(at_bottom, first_down, sent)
    both_ways(at_top, second_up, sent)
    both_ways(at_bottom, second_down, sent)
    for copy in first_sides + second_sides:
        copy.wait_send()


def relay(density_ref, accel_ref, density_out, accel_out):
    density_out[...] = density_ref[...]
    accel_out[...] = accel_ref[...]


def local(n, m, position, velocity, particle_mass, cell_counts, shear_shift):
    rows, cols, slots, _ = position.shape
    f32, bf16 = jnp.float32, jnp.bfloat16
    vmem = pl.BlockSpec(memory_space=pltpu.VMEM)
    smem = pl.BlockSpec(memory_space=pltpu.SMEM)
    cells = rows * cols
    dma = pltpu.SemaphoreType.DMA
    pair_rows = 9 * slots
    density, accel = pl.pallas_call(
        functools.partial(kernel, n, m),
        out_shape=(
            jax.ShapeDtypeStruct((rows, cols, slots), f32),
            jax.ShapeDtypeStruct((rows, 3, cols, slots), f32),
        ),
        in_specs=[vmem, vmem, vmem, smem, smem],
        out_specs=(vmem, vmem),
        scratch_shapes=[
            pltpu.VMEM((rows, cols, 8, slots), f32),
            pltpu.VMEM((3 * cols, 8, slots), f32),
            pltpu.VMEM((3 * cols, 8, slots), f32),
            pltpu.VMEM((rows, 8, slots), f32),
            pltpu.VMEM((rows, 8, slots), f32),
            pltpu.VMEM((rows + 2, cols + 2, 8, slots), f32),
            pltpu.VMEM((rows, cols, 1, slots), f32),
            pltpu.VMEM((3 * cols, 1, slots), f32),
            pltpu.VMEM((3 * cols, 1, slots), f32),
            pltpu.VMEM((rows, 1, slots), f32),
            pltpu.VMEM((rows, 1, slots), f32),
            pltpu.VMEM((rows + 2, cols + 2, 1, slots), f32),
            pltpu.VMEM((rows + 2, cols + 2, slots, FEATURES), bf16),
            pltpu.VMEM((rows + 2, cols + 2, slots, slots), f32),
            pltpu.VMEM((rows + 2, cols + 2, 8, slots), f32),
            pltpu.VMEM((rows + 2, cols + 2, 8, slots), f32),
            pltpu.VMEM((rows + 2, cols + 2, 8, slots), f32),
            pltpu.VMEM((rows, cols, 8, slots), f32),
            pltpu.VMEM((cells, 2 * pair_rows, slots), bf16),
            pltpu.VMEM((cells, pair_rows, slots), bf16),
            dma((8,)),
            dma((8,)),
            dma((8,)),
            dma((8,)),
        ],
        compiler_params=pltpu.CompilerParams(collective_id=0, has_side_effects=True),
    )(
        jnp.transpose(position, (0, 3, 1, 2)),
        jnp.transpose(velocity, (0, 3, 1, 2)),
        particle_mass,
        cell_counts,
        shear_shift,
    )
    density, accel = pl.pallas_call(
        relay,
        out_shape=(
            jax.ShapeDtypeStruct((rows, cols, slots), f32),
            jax.ShapeDtypeStruct((rows, 3, cols, slots), f32),
        ),
        in_specs=[vmem, vmem],
        out_specs=(vmem, vmem),
    )(density, accel)
    return density, jnp.transpose(accel, (0, 2, 3, 1))


def solution(mesh):
    placed = (
        P("gy", "gx", None, None),
        P("gy", "gx", None, None),
        P("gy", "gx", None),
        P("gy", "gx"),
        P(),
    )
    return jax.shard_map(
        functools.partial(local, mesh.shape["gx"], mesh.shape["gy"]),
        mesh=mesh,
        in_specs=placed,
        out_specs=(P("gy", "gx", None), P("gy", "gx", None, None)),
        check_vma=False,
    )
```

profile of v0, /device:TPU:0, one launch (start us, length us, event | category | flops | bytes accessed | tf_op | source)
XLA Modules:
  0.0 25.9 jit_solution(2281904818698620627)
XLA Ops:
  1.3 23.3 %shard_map.68 = (f32[2,8,128]{2,1,0:T(8,128)}, f32[2,3,8,128]{3,2,1,0:T(8,128)}) custom-call(f32[2,3,8,128]{3,2,1,0:T(8,128)} %bitcast.3, f32[2,3,8,128]{3,2,1,0:T(8,128)} %bitcast.4, f32[2,8,128]{2,1,0:T(8,128)} %mass_ref.1, s32[2,8]{1,0:T(2,128)} %counts_ref.1, s32[1]{0:T(128)S(6)} %copy.7.shift_ref), custom_call_target="tpu_custom_call" | custom-call | tf_op jit(solution)/shard_map/pallas_call | solution.py:364
  24.6 1.4 %shard_map.69 = (f32[2,8,128]{2,1,0:T(8,128)}, f32[2,3,8,128]{3,2,1,0:T(8,128)}) custom-call(f32[2,8,128]{2,1,0:T(8,128)} %get-tuple-element.6.density_ref, f32[2,3,8,128]{3,2,1,0:T(8,128)} %get-tuple-element.7.accel_ref), custom_call_target="tpu_custom_call" | custom-call | tf_op jit(solution)/shard_map/pallas_call | solution.py:406
where the time goes:
time: 26.2 us; the launch traced here: 25.9 us
  Pallas kernels  24.7 us (94%)
  between operations  1.29 us (5%)
    pallas_call x1, Pallas kernels, local(): pl.pallas_call(functools.partial(kernel, n, m), out_shape=(jax.ShapeDtype...  23.3 us
    pallas_call x1, Pallas kernels, local(): pl.pallas_call(relay, out_shape=(jax.ShapeDtypeStruct((rows, cols, slots)...  1.37 us

commit v1 on v0

--- a/solution.py
+++ b/solution.py
@@ -21,6 +21,8 @@
 SOFT_Q = SOFTENING / (SMOOTHING * SMOOTHING)
 TINY = 1e-10
 FEATURES = 48
+VMEM_LIMIT = 40 * 1024 * 1024
+RELAY_LIMIT = 4 * 1024 * 1024
 
 
 def split3(p):
@@ -40,11 +42,12 @@
 
 
 def kernel(
-    n, m, pos_ref, vel_ref, mass_ref, counts_ref, shift_ref, dens_ref, acc_ref,
+    n, m, pos_hbm, vel_hbm, mass_hbm, counts_hbm, shift_ref, dens_ref, acc_ref,
+    pos_ref, vel_ref, mass_ref, counts_ref,
     own, above, below, left, right, pad,
     rho, rho_above, rho_below, rho_left, rho_right, rho_pad,
     feat, mass_wide, moments, flows, wides, partial, g_pairs, l_pairs,
-    send_sem, recv_sem, rho_send_sem, rho_recv_sem,
+    send_sem, recv_sem, rho_send_sem, rho_recv_sem, load_sem,
 ):
     rows, _, cols, slots = pos_ref.shape
     gy, gx = lax.axis_index("gy"), lax.axis_index("gx")
@@ -112,6 +115,18 @@
     barrier = pltpu.get_barrier_semaphore()
     for device in partners:
         pl.semaphore_signal(barrier, inc=1, device_id=device, device_id_type=MESH)
+
+    loads = [
+        pltpu.make_async_copy(src, dst, load_sem.at[i])
+        for i, (src, dst) in enumerate([
+            (pos_hbm, pos_ref), (vel_hbm, vel_ref), (mass_hbm, mass_ref),
+            (counts_hbm, counts_ref),
+        ])
+    ]
+    for load in loads:
+        load.start()
+    for load in loads:
+        load.wait()
 
     lane = lax.broadcasted_iota(jnp.int32, (1, slots), 1)
     for r in range(rows):
@@ -348,9 +363,13 @@
         copy.wait_send()
 
 
-def relay(density_ref, accel_ref, density_out, accel_out):
-    density_out[...] = density_ref[...]
-    accel_out[...] = accel_ref[...]
+def relay(density_ref, accel_ref, density_out, accel_out, sem):
+    first = pltpu.make_async_copy(density_ref, density_out, sem.at[0])
+    second = pltpu.make_async_copy(accel_ref, accel_out, sem.at[1])
+    first.start()
+    second.start()
+    first.wait()
+    second.wait()
 
 
 def local(n, m, position, velocity, particle_mass, cell_counts, shear_shift):
@@ -358,18 +377,23 @@
     f32, bf16 = jnp.float32, jnp.bfloat16
     vmem = pl.BlockSpec(memory_space=pltpu.VMEM)
     smem = pl.BlockSpec(memory_space=pltpu.SMEM)
+    hbm = pl.BlockSpec(memory_space=pltpu.HBM)
     cells = rows * cols
     dma = pltpu.SemaphoreType.DMA
     pair_rows = 9 * slots
     density, accel = pl.pallas_call(
         functools.partial(kernel, n, m),
         out_shape=(
-            jax.ShapeDtypeStruct((rows, cols, slots), f32),
-            jax.ShapeDtypeStruct((rows, 3, cols, slots), f32),
+            pltpu.VMEM((rows, cols, slots), f32),
+            pltpu.VMEM((rows, 3, cols, slots), f32),
         ),
-        in_specs=[vmem, vmem, vmem, smem, smem],
+        in_specs=[hbm] * 4 + [smem],
         out_specs=(vmem, vmem),
         scratch_shapes=[
+            pltpu.VMEM((rows, 3, cols, slots), f32),
+            pltpu.VMEM((rows, 3, cols, slots), f32),
+            pltpu.VMEM((rows, cols, slots), f32),
+            pltpu.SMEM((rows, cols), jnp.int32),
             pltpu.VMEM((rows, cols, 8, slots), f32),
             pltpu.VMEM((3 * cols, 8, slots), f32),
             pltpu.VMEM((3 * cols, 8, slots), f32),
@@ -394,13 +418,21 @@
             dma((8,)),
             dma((8,)),
             dma((8,)),
+            dma((4,)),
         ],
-        compiler_params=pltpu.CompilerParams(collective_id=0, has_side_effects=True),
+        compiler_params=pltpu.CompilerParams(
+            collective_id=0, has_side_effects=True, vmem_limit_bytes=VMEM_LIMIT
+        ),
     )(
-        jnp.transpose(position, (0, 3, 1, 2)),
-        jnp.transpose(velocity, (0, 3, 1, 2)),
-        particle_mass,
-        cell_counts,
+        *(
+            pltpu.with_memory_space_constraint(operand, pltpu.HBM)
+            for operand in (
+                jnp.transpose(position, (0, 3, 1, 2)),
+                jnp.transpose(velocity, (0, 3, 1, 2)),
+                particle_mass,
+                cell_counts,
+            )
+        ),
         shear_shift,
     )
     density, accel = pl.pallas_call(
@@ -410,7 +442,9 @@
             jax.ShapeDtypeStruct((rows, 3, cols, slots), f32),
         ),
         in_specs=[vmem, vmem],
-        out_specs=(vmem, vmem),
+        out_specs=(hbm, hbm),
+        scratch_shapes=[dma((2,))],
+        compiler_params=pltpu.CompilerParams(vmem_limit_bytes=RELAY_LIMIT),
     )(density, accel)
     return density, jnp.transpose(accel, (0, 2, 3, 1))
 

time: 26.2 us -> 24 us (0.916)
  Pallas kernels: 24.7 us -> 22.5 us
    pallas_call x1, Pallas kernels: 23.3 us -> 21.9 us  [local(): pl.pallas_call(functools.partial(kernel, n, m), out_shape=(pltpu.VMEM((ro...]
    pallas_call x1, Pallas kernels: 1.37 us -> 0.63 us  [local(): pl.pallas_call(relay, out_shape=(jax.ShapeDtypeStruct((rows, cols, slots)...]
where the time goes in v1:
time: 24 us; the launch traced here: 23.8 us
  Pallas kernels  22.5 us (94%)
  between operations  1.29 us (5%)
    pallas_call x1, Pallas kernels, local(): pl.pallas_call(functools.partial(kernel, n, m), out_shape=(pltpu.VMEM((ro...  21.9 us
    pallas_call x1, Pallas kernels, local(): pl.pallas_call(relay, out_shape=(jax.ShapeDtypeStruct((rows, cols, slots)...  0.63 us

profile of v1, /device:TPU:0, one launch (start us, length us, event | category | flops | bytes accessed | tf_op | source)
XLA Modules:
  0.0 23.8 jit_solution(17197120087733737964)
XLA Ops:
  1.3 21.9 %shard_map.68 = (f32[2,8,128]{2,1,0:T(8,128)S(1)}, f32[2,3,8,128]{3,2,1,0:T(8,128)S(1)}) custom-call(f32[2,3,8,128]{3,2,1,0:T(8,128)} %bitcast.3, f32[2,3,8,128]{3,2,1,0:T(8,128)} %bitcast.4, f32[2,8,128]{2,1,0:T(8,128)} %mass_hbm.1, s32[2,8]{1,0:T(2,128)} %counts_hbm.1, s32[1]{0:T(128)S(6)} %copy.7.shift_ref), custom_call_target="tpu_custom_call" | custom-call | tf_op jit(solution)/shard_map/pallas_call | solution.py:384
  23.2 0.6 %shard_map.69 = (f32[2,8,128]{2,1,0:T(8,128)}, f32[2,3,8,128]{3,2,1,0:T(8,128)}) custom-call(f32[2,8,128]{2,1,0:T(8,128)S(1)} %get-tuple-element.6.density_ref, f32[2,3,8,128]{3,2,1,0:T(8,128)S(1)} %get-tuple-element.7.accel_ref), custom_call_target="tpu_custom_call" | custom-call | tf_op jit(solution)/shard_map/pallas_call | solution.py:438

commit v2 on v1

--- a/solution.py
+++ b/solution.py
@@ -46,7 +46,7 @@
     pos_ref, vel_ref, mass_ref, counts_ref,
     own, above, below, left, right, pad,
     rho, rho_above, rho_below, rho_left, rho_right, rho_pad,
-    feat, mass_wide, moments, flows, wides, partial, g_pairs, l_pairs,
+    feat, mass_wide, moments, flows, wides, partial, force_sum, g_pairs, l_pairs,
     send_sem, recv_sem, rho_send_sem, rho_recv_sem, load_sem,
 ):
     rows, _, cols, slots = pos_ref.shape
@@ -64,6 +64,19 @@
     partners += [(down, beside(off_down, k)) for k in (-1, 0, 1)]
     partners += [(gy, beside(0, k)) for k in (-1, 1)]
 
+    barrier = pltpu.get_barrier_semaphore()
+    for device in partners:
+        pl.semaphore_signal(barrier, inc=1, device_id=device, device_id_type=MESH)
+    loads = [
+        pltpu.make_async_copy(src, dst, load_sem.at[i])
+        for i, (src, dst) in enumerate([
+            (pos_hbm, pos_ref), (vel_hbm, vel_ref), (mass_hbm, mass_ref),
+            (counts_hbm, counts_ref),
+        ])
+    ]
+    for load in loads:
+        load.start()
+
     def copy_to(src, dst, sends, recvs, i, device):
         return pltpu.make_async_remote_copy(
             src_ref=src, dst_ref=dst, send_sem=sends.at[i], recv_sem=recvs.at[i],
@@ -91,6 +104,10 @@
             for copy in make(False):
                 act(copy)
 
+    def either(choice, one, other):
+        pl.when(choice)(one)
+        pl.when(jnp.logical_not(choice))(other)
+
     def start(copy):
         copy.start()
 
@@ -112,40 +129,17 @@
             copy_to(mine.at[:, cols - 1], from_left, sends, recvs, 7, (gy, beside(0, -1))),
         ]
 
-    barrier = pltpu.get_barrier_semaphore()
-    for device in partners:
-        pl.semaphore_signal(barrier, inc=1, device_id=device, device_id_type=MESH)
-
-    loads = [
-        pltpu.make_async_copy(src, dst, load_sem.at[i])
-        for i, (src, dst) in enumerate([
-            (pos_hbm, pos_ref), (vel_hbm, vel_ref), (mass_hbm, mass_ref),
-            (counts_hbm, counts_ref),
-        ])
-    ]
-    for load in loads:
-        load.start()
-    for load in loads:
-        load.wait()
-
-    lane = lax.broadcasted_iota(jnp.int32, (1, slots), 1)
-    for r in range(rows):
-        for c in range(cols):
-            for k in range(3):
-                own[r, c, pl.ds(k, 1), :] = pos_ref[r, k, pl.ds(c, 1), :]
-                own[r, c, pl.ds(3 + k, 1), :] = vel_ref[r, k, pl.ds(c, 1), :]
-            w = jnp.where(lane < counts_ref[r, c], mass_ref[r, pl.ds(c, 1), :], 0.0)
-            own[r, c, pl.ds(6, 1), :] = w
-            own[r, c, pl.ds(7, 1), :] = jnp.zeros_like(w)
-
-    pl.semaphore_wait(barrier, len(partners))
     first_up = to_up(own, below, send_sem, recv_sem)
     first_down = to_down(own, above, send_sem, recv_sem)
     first_sides = to_sides(own, left, right, send_sem, recv_sem)
-    both_ways(at_top, first_up, start)
-    both_ways(at_bottom, first_down, start)
-    for copy in first_sides:
-        copy.start()
+    second_up = to_up(rho, rho_below, rho_send_sem, rho_recv_sem)
+    second_down = to_down(rho, rho_above, rho_send_sem, rho_recv_sem)
+    second_sides = to_sides(rho, rho_left, rho_right, rho_send_sem, rho_recv_sem)
+
+    last = rows - 1
+    near_row = jnp.where(at_top, 0, last)
+    far_row = last - near_row
+    turn = jnp.where(gx == 0, jnp.where(gy == 0, 2, jnp.where(gy == 1, 2, 0)), 0)
 
     shift = shift_ref[0]
     total_half = half * cols
@@ -191,15 +185,25 @@
             prepare(r + 1, c + 1, own[r, c])
         return carry
 
-    lax.fori_loop(0, rows, prepare_row, 0)
-
-    near = [(a, b) for a in (-1, 0, 1) for b in (-1, 0, 1)]
+    def outward(r):
+        return jnp.where(r == 0, -1, 1)
+
+    def rows_of(r):
+        out = outward(r)
+        return (out, 0, -out)
+
+    inside = [(role, b) for role in (1, 2) for b in (-1, 0, 1)]
+    beyond = [(0, b) for b in (-1, 0, 1)]
 
     def add_pairs(r, c, total, pairs):
         i = r * cols + c
         x = 2.0 * pad[r + 1, c + 1] - 1.0
-        for a, b in pairs:
-            offset = jnp.where(row8 == 0, 2.0 * b, jnp.where(row8 == 1, 2.0 * a, 0.0))
+        steps = rows_of(r)
+        for role, b in pairs:
+            a = steps[role]
+            rise = 2.0 * jnp.asarray(a, jnp.float32)
+            run = 2.0 * jnp.asarray(b, jnp.float32)
+            offset = jnp.where(row8 == 0, run, jnp.where(row8 == 1, rise, 0.0))
             u = jnp.where(row8 < 3, x - offset, 0.0)
             norm = jnp.sum(u * u, axis=0, keepdims=True)
             p = jnp.where(row8 == 3, 1.0, -2.0 * u)
@@ -207,26 +211,23 @@
             h, mid, low = split3(p)
             stacked = jnp.concatenate([h, mid, h, low, h, mid], axis=0).astype(jnp.bfloat16)
             s = dot(feat[r + 1 + a, c + 1 + b], stacked)
-            s = jnp.maximum(s, TINY)
+            s = jnp.clip(s, TINY, 4.0)
             inv = lax.rsqrt(s)
             q = s * inv
             outer = 2.0 - q
             inner = jnp.maximum(outer - q, 0.0)
-            outer = jnp.maximum(outer, 0.0)
             inner_sq = inner * inner
             slope = outer * outer - inner_sq
             value = (outer * slope + inner_sq) * mass_wide[r + 1 + a, c + 1 + b]
             total = total + jnp.sum(value.reshape(slots // 8, 8, slots), axis=0)
             g = slope * inv
-            index = near.index((a, b))
             g_high = g.astype(jnp.bfloat16)
-            g_pairs[i, pl.ds(index * 2 * slots, slots), :] = g_high
-            g_pairs[i, pl.ds(index * 2 * slots + slots, slots), :] = (
+            place = role * 3 + b + 1
+            g_pairs[i, place, pl.ds(0, slots)] = g_high
+            g_pairs[i, place, pl.ds(slots, slots)] = (
                 g - g_high.astype(jnp.float32)
             ).astype(jnp.bfloat16)
-            l_pairs[i, pl.ds(index * slots, slots), :] = (g * (1.0 / (s + SOFT_Q))).astype(
-                jnp.bfloat16
-            )
+            l_pairs[i, place] = (g * (1.0 / (s + SOFT_Q))).astype(jnp.bfloat16)
         return total
 
     zero8 = jnp.zeros((8, slots), jnp.float32)
@@ -235,126 +236,192 @@
         row = W_SCALE * jnp.sum(total, axis=0, keepdims=True)
         occupied = pad[r + 1, c + 1, 6:7] > 0.0
         dens_ref[r, pl.ds(c, 1), :] = jnp.where(occupied, row, 0.0)
-        rho[r, c] = 1.0 / jnp.where(occupied, row, 1.0)
-
-    def near_own(r):
-        return [(a, b) for a, b in near if 0 <= r + a < rows]
-
-    def near_ghost(r):
-        return [(a, b) for a, b in near if not 0 <= r + a < rows]
-
-    def density_own(r):
-        def step(c, carry):
-            partial[r, c] = add_pairs(r, c, zero8, near_own(r))
-            return carry
-
-        lax.fori_loop(1, cols - 1, step, 0, unroll=3)
-
-    def density_ghost(r):
-        def step(c, carry):
-            finish(r, c, add_pairs(r, c, partial[r, c], near_ghost(r)))
-            return carry
-
-        lax.fori_loop(1, cols - 1, step, 0, unroll=3)
-
-        def edge(k, carry):
-            c = k * (cols - 1)
-            finish(r, c, add_pairs(r, c, zero8, near))
-            return carry
-
-        lax.fori_loop(0, 2, edge, 0, unroll=2)
-
+        inverse = 1.0 / jnp.where(occupied, row, 1.0)
+        rho[r, c] = inverse
+        rho_pad[r + 1, c + 1] = inverse
+
+    def edge_pairs(c, pairs, sideways):
+        if c in (0, cols - 1):
+            out = -1 if c == 0 else 1
+            return [(role, b) for role, b in pairs if b != out] if not sideways else pairs + [(1, out), (2, out)]
+        return pairs
+
+    def own_row(r):
+        for c in range(cols):
+            partial[r, c] = add_pairs(r, c, zero8, edge_pairs(c, inside, False))
+
+    def ghost_density(r):
+        for c in range(cols):
+            finish(r, c, add_pairs(r, c, partial[r, c], edge_pairs(c, beyond, True)))
+
+    for load in loads:
+        load.wait()
+    lane = lax.broadcasted_iota(jnp.int32, (1, slots), 1)
     for r in range(rows):
-        density_own(r)
-
-    both_ways(at_bottom, first_up, received)
-    both_ways(at_top, first_down, received)
-    for copy in first_sides:
-        copy.wait_recv()
-    for r in range(rows):
-        prepare(r + 1, 0, left[r])
-        prepare(r + 1, cols + 1, right[r])
-
-    for t in range(wide):
-        prepare(0, t, below[start_below + t] - jump_below)
-    for t in range(wide):
-        prepare(rows + 1, t, above[start_above + t] + jump_above)
-
-    second_up = to_up(rho, rho_below, rho_send_sem, rho_recv_sem)
-    second_down = to_down(rho, rho_above, rho_send_sem, rho_recv_sem)
-    second_sides = to_sides(rho, rho_left, rho_right, rho_send_sem, rho_recv_sem)
-    density_ghost(0)
-    both_ways(at_bottom, second_down, start)
-    for r in range(1, rows):
-        density_ghost(r)
-    both_ways(at_top, second_up, start)
+        for c in range(cols):
+            for k in range(3):
+                own[r, c, pl.ds(k, 1), :] = pos_ref[r, k, pl.ds(c, 1), :]
+                own[r, c, pl.ds(3 + k, 1), :] = vel_ref[r, k, pl.ds(c, 1), :]
+            w = jnp.where(lane < counts_ref[r, c], mass_ref[r, pl.ds(c, 1), :], 0.0)
+            own[r, c, pl.ds(6, 1), :] = w
+            own[r, c, pl.ds(7, 1), :] = jnp.zeros_like(w)
+
+    def send_fields(low_first):
+        def send():
+            if low_first:
+                both_ways(at_bottom, first_down, start)
+            both_ways(at_top, first_up, start)
+            if not low_first:
+                both_ways(at_bottom, first_down, start)
+
+        return send
+
+    def send_stage(stage):
+        @pl.when(turn == stage)
+        def _():
+            pl.semaphore_wait(barrier, len(partners))
+            either(at_bottom, send_fields(True), send_fields(False))
+            for copy in first_sides:
+                copy.start()
+
+    def own_step(t, carry):
+        @pl.when(t == 1)
+        def _():
+            send_stage(1)
+
+        own_row(t * last)
+        return carry
+
+    with jax.named_scope("send0"):
+        send_stage(0)
+    with jax.named_scope("prepown"):
+        lax.fori_loop(0, rows, prepare_row, 0)
+    with jax.named_scope("own"):
+        lax.fori_loop(0, 2, own_step, 0)
+    with jax.named_scope("send2"):
+        send_stage(2)
+
+    def fields_below():
+        both_ways(at_bottom, first_up, received)
+        for t in range(wide):
+            pad[0, t] = below[start_below + t] - jump_below
+
+    def fields_above():
+        both_ways(at_top, first_down, received)
+        for t in range(wide):
+            pad[rows + 1, t] = above[start_above + t] + jump_above
+
+    def prepare_ghosts(r):
+        p = r + 1 + outward(r)
+        for t in range(wide):
+            prepare(p, t, pad[p, t])
+
+    with jax.named_scope("recvside"):
+        for copy in first_sides:
+            copy.wait_recv()
+    with jax.named_scope("recvnear"):
+        either(at_top, fields_below, fields_above)
+    with jax.named_scope("near"):
+        for r in range(rows):
+            prepare(r + 1, 0, left[r])
+            prepare(r + 1, cols + 1, right[r])
+        prepare_ghosts(near_row)
+        ghost_density(near_row)
+    either(
+        at_top,
+        lambda: both_ways(at_bottom, second_down, start),
+        lambda: both_ways(at_top, second_up, start),
+    )
+    with jax.named_scope("recvfar"):
+        either(at_top, fields_above, fields_below)
+    with jax.named_scope("far"):
+        prepare_ghosts(far_row)
+        ghost_density(far_row)
+    either(
+        at_top,
+        lambda: both_ways(at_top, second_up, start),
+        lambda: both_ways(at_bottom, second_down, start),
+    )
     for copy in second_sides:
         copy.start()
-    for r in range(rows):
-        for c in range(cols):
-            rho_pad[r + 1, c + 1] = rho[r, c]
-    both_ways(at_top, second_down, received)
-    for t in range(wide):
-        rho_pad[rows + 1, t] = rho_above[start_above + t]
 
     upper_half = row8 >= 4
 
-    def force(r, c):
+    def push(r, c, pairs):
         i = r * cols + c
-        f = pad[r + 1, c + 1]
-        mine = rho_pad[r + 1, c + 1]
-        g_lhs, k_lhs = [], []
-        for a, b in near:
-            inverse = jnp.broadcast_to(rho_pad[r + 1 + a, c + 1 + b], f.shape)
+        steps = rows_of(r)
+        g_lhs, k_lhs, g_rhs, l_rhs = [], [], [], []
+        for role, b in pairs:
+            a = steps[role]
+            inverse = jnp.broadcast_to(rho_pad[r + 1 + a, c + 1 + b], (8, slots))
             w = wides[r + 1 + a, c + 1 + b]
             moment = moments[r + 1 + a, c + 1 + b]
-            offset = jnp.where(row8 % 4 == 1, float(b), jnp.where(row8 % 4 == 2, float(a), 0.0))
+            rise = jnp.asarray(a, jnp.float32)
+            offset = jnp.where(row8 % 4 == 1, float(b), jnp.where(row8 % 4 == 2, rise, 0.0))
             moment = moment + offset * w
             g_rows = split2(jnp.where(upper_half, moment * inverse, moment))
             k_rows = split2(flows[r + 1 + a, c + 1 + b] * inverse)
             both = jnp.concatenate([g_rows, k_rows], axis=0)
             g_lhs += [both, both]
             k_lhs.append(k_rows)
-        sums = dot(jnp.concatenate(g_lhs, axis=1), g_pairs[i])
-        soft = dot(jnp.concatenate(k_lhs, axis=1), l_pairs[i])
+            place = role * 3 + b + 1
+            g_rhs.append(g_pairs[i, place])
+            l_rhs.append(l_pairs[i, place])
+        sums = dot(jnp.concatenate(g_lhs, axis=1), jnp.concatenate(g_rhs, axis=0))
+        soft = dot(jnp.concatenate(k_lhs, axis=1), jnp.concatenate(l_rhs, axis=0))
         g_sum = sums[0:8] + sums[8:16]
         k_sum = (sums[16:24] + sums[24:32]) - SOFT_Q * (soft[0:8] + soft[8:16])
+        return jnp.concatenate([g_sum, k_sum], axis=0)
+
+    def settle(r, c, sums):
+        f = pad[r + 1, c + 1]
+        mine = rho_pad[r + 1, c + 1]
         here = f[0:3] - 0.5
-        plain = here * g_sum[0:1] - g_sum[1:4]
-        weighed = here * g_sum[4:5] - g_sum[5:8]
+        plain = here * sums[0:1] - sums[1:4]
+        weighed = here * sums[4:5] - sums[5:8]
         pressure = -SOUND_SQ * (mine * plain + weighed)
-        viscous = (2.0 * VISCOSITY) * mine * (f[3:6] * k_sum[0:1] - k_sum[1:4])
+        viscous = (2.0 * VISCOSITY) * mine * (f[3:6] * sums[8:9] - sums[9:12])
         accel = jnp.where(f[6:7] > 0.0, G_SCALE * (pressure + viscous), 0.0)
         for k in range(3):
             acc_ref[r, k, pl.ds(c, 1), :] = accel[k : k + 1]
 
-    def force_inner(c, carry):
-        force(rows - 1, 2 * c + 1)
-        force(rows - 1, 2 * c + 2)
+    def own_force(t, carry):
+        r = t * last
+        for c in range(cols):
+            force_sum[r, c] = push(r, c, edge_pairs(c, inside, False))
         return carry
 
-    early = (cols - 2) // 2 if rows > 1 else 0
-    lax.fori_loop(0, early, force_inner, 0)
-
-    both_ways(at_bottom, second_up, received)
-    for copy in second_sides:
-        copy.wait_recv()
+    with jax.named_scope("ownforce"):
+        lax.fori_loop(0, 2, own_force, 0)
+
+    def ghost_force(r):
+        for c in range(cols):
+            settle(r, c, force_sum[r, c] + push(r, c, edge_pairs(c, beyond, True)))
+
+    def rho_from_below():
+        both_ways(at_bottom, second_up, received)
+        for t in range(wide):
+            rho_pad[0, t] = rho_below[start_below + t]
+
+    def rho_from_above():
+        both_ways(at_top, second_down, received)
+        for t in range(wide):
+            rho_pad[rows + 1, t] = rho_above[start_above + t]
+
+    with jax.named_scope("rhoside"):
+        for copy in second_sides:
+            copy.wait_recv()
     for r in range(rows):
         rho_pad[r + 1, 0] = rho_left[r]
         rho_pad[r + 1, cols + 1] = rho_right[r]
-    for t in range(wide):
-        rho_pad[0, t] = rho_below[start_below + t]
-
-    force(rows - 1, 0)
-    for c in range(2 * early + 1, cols):
-        force(rows - 1, c)
-
-    def force_pair(i, carry):
-        force(i // (cols // 2), 2 * (i % (cols // 2)))
-        force(i // (cols // 2), 2 * (i % (cols // 2)) + 1)
-        return carry
-
-    lax.fori_loop(0, (rows - 1) * (cols // 2), force_pair, 0)
+    with jax.named_scope("rhonear"):
+        either(at_top, rho_from_below, rho_from_above)
+    with jax.named_scope("nearforce"):
+        ghost_force(near_row)
+    with jax.named_scope("rhofar"):
+        either(at_top, rho_from_above, rho_from_below)
+    with jax.named_scope("farforce"):
+        ghost_force(far_row)
     both_ways(at_top, first_up, sent)
     both_ways(at_bottom, first_down, sent)
     both_ways(at_top, second_up, sent)
@@ -380,7 +447,6 @@
     hbm = pl.BlockSpec(memory_space=pltpu.HBM)
     cells = rows * cols
     dma = pltpu.SemaphoreType.DMA
-    pair_rows = 9 * slots
     density, accel = pl.pallas_call(
         functools.partial(kernel, n, m),
         out_shape=(
@@ -412,8 +478,9 @@
             pltpu.VMEM((rows + 2, cols + 2, 8, slots), f32),
             pltpu.VMEM((rows + 2, cols + 2, 8, slots), f32),
             pltpu.VMEM((rows, cols, 8, slots), f32),
-            pltpu.VMEM((cells, 2 * pair_rows, slots), bf16),
-            pltpu.VMEM((cells, pair_rows, slots), bf16),
+            pltpu.VMEM((rows, cols, 16, slots), f32),
+            pltpu.VMEM((cells, 9, 2 * slots, slots), bf16),
+            pltpu.VMEM((cells, 9, slots, slots), bf16),
             dma((8,)),
             dma((8,)),
             dma((8,)),

time: 24 us -> 21.6 us (0.900)
  Pallas kernels: 22.5 us -> 20.2 us
    pallas_call x1, Pallas kernels: 21.9 us -> 19.5 us  [local(): pl.pallas_call(functools.partial(kernel, n, m), out_shape=(pltpu.VMEM((ro...]
where the time goes in v2:
time: 21.6 us; the launch traced here: 21.4 us
  Pallas kernels  20.2 us (94%)
  between operations  1.29 us (6%)
    pallas_call x1, Pallas kernels, local(): pl.pallas_call(functools.partial(kernel, n, m), out_shape=(pltpu.VMEM((ro...  19.5 us
    pallas_call x1, Pallas kernels, local(): pl.pallas_call(relay, out_shape=(jax.ShapeDtypeStruct((rows, cols, slots)...  0.63 us

profile of v2, /device:TPU:0, one launch (start us, length us, event | category | flops | bytes accessed | tf_op | source)
XLA Modules:
  0.0 21.4 jit_solution(5769263752703943380)
XLA Ops:
  1.3 19.5 %shard_map.68 = (f32[2,8,128]{2,1,0:T(8,128)S(1)}, f32[2,3,8,128]{3,2,1,0:T(8,128)S(1)}) custom-call(f32[2,3,8,128]{3,2,1,0:T(8,128)} %bitcast.3, f32[2,3,8,128]{3,2,1,0:T(8,128)} %bitcast.4, f32[2,8,128]{2,1,0:T(8,128)} %mass_hbm.1, s32[2,8]{1,0:T(2,128)} %counts_hbm.1, s32[1]{0:T(128)S(6)} %copy.7.shift_ref), custom_call_target="tpu_custom_call" | custom-call | tf_op jit(solution)/shard_map/pallas_call | solution.py:450
  20.8 0.6 %shard_map.69 = (f32[2,8,128]{2,1,0:T(8,128)}, f32[2,3,8,128]{3,2,1,0:T(8,128)}) custom-call(f32[2,8,128]{2,1,0:T(8,128)S(1)} %get-tuple-element.6.density_ref, f32[2,3,8,128]{3,2,1,0:T(8,128)S(1)} %get-tuple-element.7.accel_ref), custom_call_target="tpu_custom_call" | custom-call | tf_op jit(solution)/shard_map/pallas_call | solution.py:505

commit v3 on v2

--- a/solution.py
+++ b/solution.py
@@ -21,6 +21,7 @@
 SOFT_Q = SOFTENING / (SMOOTHING * SMOOTHING)
 TINY = 1e-10
 FEATURES = 48
+PLACES = 11
 VMEM_LIMIT = 40 * 1024 * 1024
 RELAY_LIMIT = 4 * 1024 * 1024
 
@@ -46,7 +47,8 @@
     pos_ref, vel_ref, mass_ref, counts_ref,
     own, above, below, left, right, pad,
     rho, rho_above, rho_below, rho_left, rho_right, rho_pad,
-    feat, mass_wide, moments, flows, wides, partial, force_sum, g_pairs, l_pairs,
+    feat, mass_wide, moments, flows, wides, run_rows, rise_rows, partial, backward, force_sum,
+    g_pairs, l_pairs,
     send_sem, recv_sem, rho_send_sem, rho_recv_sem, load_sem,
 ):
     rows, _, cols, slots = pos_ref.shape
@@ -83,9 +85,9 @@
             device_id=device, device_id_type=MESH,
         )
 
-    def rows_to(mine_row, ghost, sends, recvs, base, slab, off, full):
+    def rows_to(mine_row, ghost, sends, recvs, base, slab, off, full, only):
         copies = []
-        for k in (-1, 0, 1):
+        for k in only:
             count = cols if k == 0 else reach + 1 if full else 1
             edge = cols - count if k == -1 else 0
             src = mine_row.at[pl.ds(edge, count)]
@@ -118,10 +120,14 @@
         copy.wait_recv()
 
     def to_up(mine, ghost, sends, recvs):
-        return lambda full: rows_to(mine.at[rows - 1], ghost, sends, recvs, 0, up, off_up, full)
+        return lambda full, only=(-1, 0, 1): rows_to(
+            mine.at[rows - 1], ghost, sends, recvs, 0, up, off_up, full, only
+        )
 
     def to_down(mine, ghost, sends, recvs):
-        return lambda full: rows_to(mine.at[0], ghost, sends, recvs, 3, down, off_down, full)
+        return lambda full, only=(-1, 0, 1): rows_to(
+            mine.at[0], ghost, sends, recvs, 3, down, off_down, full, only
+        )
 
     def to_sides(mine, from_left, from_right, sends, recvs):
         return [
@@ -139,7 +145,7 @@
     last = rows - 1
     near_row = jnp.where(at_top, 0, last)
     far_row = last - near_row
-    turn = jnp.where(gx == 0, jnp.where(gy == 0, 2, jnp.where(gy == 1, 2, 0)), 0)
+    turn = jnp.where(gx == 0, 2, 0)
 
     shift = shift_ref[0]
     total_half = half * cols
@@ -180,54 +186,68 @@
         flows[r, c] = jnp.where(row8 < 4, flow, 0.0) * w
         wides[r, c] = w
 
-    def prepare_row(r, carry):
-        for c in range(cols):
-            prepare(r + 1, c + 1, own[r, c])
-        return carry
+    def prepare_own(r, c):
+        f = own[r, c]
+        prepare(r + 1, c + 1, f)
+        x = 2.0 * f - 1.0
+        for k in (-1, 0, 1):
+            run = x[0:1] - 2.0 * k
+            rise = x[1:2] - 2.0 * k
+            square = rise * rise + x[2:3] * x[2:3]
+            across = jnp.where(row8 == 4, run * run, jnp.where(row8 == 0, 4.0 * k, 0.0))
+            along = jnp.where(row8 == 4, square, jnp.where(row8 < 3, -2.0 * x, 0.0))
+            run_rows[r, c, k + 1] = across
+            rise_rows[r, c, k + 1] = along + jnp.where(row8 == 1, 4.0 * k, jnp.where(row8 == 3, 1.0, 0.0))
 
     def outward(r):
         return jnp.where(r == 0, -1, 1)
 
-    def rows_of(r):
-        out = outward(r)
-        return (out, 0, -out)
-
-    inside = [(role, b) for role in (1, 2) for b in (-1, 0, 1)]
-    beyond = [(0, b) for b in (-1, 0, 1)]
+    OWN = ((0, 0), (0, 1), (1, -1), (1, 0), (1, 1))
+    BEYOND, SIDE = len(OWN), len(OWN) + 3
+
+    def forward(r, c):
+        return [(a, b) for a, b in OWN if r + a < rows and 0 <= c + b < cols]
+
+    def back(r, c):
+        pairs = [(a, b) for a, b in OWN[1:] if r - a >= 0 and 0 <= c - b < cols]
+        return [(r - a, c - b, -a, -b, OWN.index((a, b))) for a, b in pairs]
+
+    def sideways(r, c):
+        if c not in (0, cols - 1):
+            return []
+        b = -1 if c == 0 else 1
+        return [(a, b, SIDE + a + 1) for a in (-1, 0, 1) if 0 <= r + a < rows]
+
+    def beyond(r):
+        return [(outward(r), b, BEYOND + b + 1) for b in (-1, 0, 1)]
+
+    def fold(x):
+        return jnp.sum(x.reshape(slots // 8, 8, slots), axis=0)
+
+    def pair(r, c, a, b, place):
+        i = r * cols + c
+        h, mid, low = split3(rise_rows[r, c, a + 1] + run_rows[r, c, b + 1])
+        stacked = jnp.concatenate([h, mid, h, low, h, mid], axis=0).astype(jnp.bfloat16)
+        s = dot(feat[r + 1 + a, c + 1 + b], stacked)
+        s = jnp.clip(s, TINY, 4.0)
+        inv = lax.rsqrt(s)
+        q = s * inv
+        outer = 2.0 - q
+        inner = jnp.maximum(outer - q, 0.0)
+        inner_sq = inner * inner
+        slope = outer * outer - inner_sq
+        g = slope * inv
+        g_high = g.astype(jnp.bfloat16)
+        g_pairs[i, place, pl.ds(0, slots)] = g_high
+        g_pairs[i, place, pl.ds(slots, slots)] = (
+            g - g_high.astype(jnp.float32)
+        ).astype(jnp.bfloat16)
+        l_pairs[i, place] = g_high / (s + SOFT_Q).astype(jnp.bfloat16)
+        return outer * slope + inner_sq
 
     def add_pairs(r, c, total, pairs):
-        i = r * cols + c
-        x = 2.0 * pad[r + 1, c + 1] - 1.0
-        steps = rows_of(r)
-        for role, b in pairs:
-            a = steps[role]
-            rise = 2.0 * jnp.asarray(a, jnp.float32)
-            run = 2.0 * jnp.asarray(b, jnp.float32)
-            offset = jnp.where(row8 == 0, run, jnp.where(row8 == 1, rise, 0.0))
-            u = jnp.where(row8 < 3, x - offset, 0.0)
-            norm = jnp.sum(u * u, axis=0, keepdims=True)
-            p = jnp.where(row8 == 3, 1.0, -2.0 * u)
-            p = jnp.where(row8 == 4, norm, p)
-            h, mid, low = split3(p)
-            stacked = jnp.concatenate([h, mid, h, low, h, mid], axis=0).astype(jnp.bfloat16)
-            s = dot(feat[r + 1 + a, c + 1 + b], stacked)
-            s = jnp.clip(s, TINY, 4.0)
-            inv = lax.rsqrt(s)
-            q = s * inv
-            outer = 2.0 - q
-            inner = jnp.maximum(outer - q, 0.0)
-            inner_sq = inner * inner
-            slope = outer * outer - inner_sq
-            value = (outer * slope + inner_sq) * mass_wide[r + 1 + a, c + 1 + b]
-            total = total + jnp.sum(value.reshape(slots // 8, 8, slots), axis=0)
-            g = slope * inv
-            g_high = g.astype(jnp.bfloat16)
-            place = role * 3 + b + 1
-            g_pairs[i, place, pl.ds(0, slots)] = g_high
-            g_pairs[i, place, pl.ds(slots, slots)] = (
-                g - g_high.astype(jnp.float32)
-            ).astype(jnp.bfloat16)
-            l_pairs[i, place] = (g * (1.0 / (s + SOFT_Q))).astype(jnp.bfloat16)
+        for a, b, place in pairs:
+            total = total + fold(pair(r, c, a, b, place) * mass_wide[r + 1 + a, c + 1 + b])
         return total
 
     zero8 = jnp.zeros((8, slots), jnp.float32)
@@ -240,19 +260,22 @@
         rho[r, c] = inverse
         rho_pad[r + 1, c + 1] = inverse
 
-    def edge_pairs(c, pairs, sideways):
-        if c in (0, cols - 1):
-            out = -1 if c == 0 else 1
-            return [(role, b) for role, b in pairs if b != out] if not sideways else pairs + [(1, out), (2, out)]
-        return pairs
-
     def own_row(r):
         for c in range(cols):
-            partial[r, c] = add_pairs(r, c, zero8, edge_pairs(c, inside, False))
-
-    def ghost_density(r):
-        for c in range(cols):
-            finish(r, c, add_pairs(r, c, partial[r, c], edge_pairs(c, beyond, True)))
+            total = zero8
+            for a, b in forward(r, c):
+                value = pair(r, c, a, b, OWN.index((a, b)))
+                total = total + fold(value * mass_wide[r + 1 + a, c + 1 + b])
+                if (a, b) != (0, 0):
+                    weighed = value.reshape(slots // 8, 8, slots) * wides[r + 1, c + 1][None]
+                    weighed = weighed.reshape(slots, slots)
+                    if (r, c) == min(back(r + a, c + b))[:2]:
+                        backward[r + a, c + b] = weighed
+                    else:
+                        backward[r + a, c + b] += weighed
+            if back(r, c):
+                total = total + fold(backward[r, c].T)
+            partial[r, c] = total
 
     for load in loads:
         load.wait()
@@ -280,98 +303,172 @@
         @pl.when(turn == stage)
         def _():
             pl.semaphore_wait(barrier, len(partners))
-            either(at_bottom, send_fields(True), send_fields(False))
             for copy in first_sides:
                 copy.start()
-
-    def own_step(t, carry):
-        @pl.when(t == 1)
-        def _():
-            send_stage(1)
-
-        own_row(t * last)
-        return carry
+            either(at_bottom, send_fields(True), send_fields(False))
 
     with jax.named_scope("send0"):
         send_stage(0)
-    with jax.named_scope("prepown"):
-        lax.fori_loop(0, rows, prepare_row, 0)
-    with jax.named_scope("own"):
-        lax.fori_loop(0, 2, own_step, 0)
+    with jax.named_scope("own0"):
+        for r in range(rows):
+            for c in range(cols):
+                prepare_own(r, c)
+        own_row(0)
+    with jax.named_scope("send1"):
+        send_stage(1)
+    with jax.named_scope("own1"):
+        for r in range(1, rows):
+            own_row(r)
     with jax.named_scope("send2"):
         send_stage(2)
 
-    def fields_below():
-        both_ways(at_bottom, first_up, received)
+    def inner_below():
+        first_up(False, (0,))[0].wait_recv()
+        for t in range(1, wide - 1):
+            pad[0, t] = below[cols - 1 + t]
+
+    def inner_above():
+        first_down(False, (0,))[0].wait_recv()
+        for t in range(1, wide - 1):
+            pad[rows + 1, t] = above[cols - 1 + t]
+
+    def outer_below():
+        for copy in first_up(False, (-1, 1)):
+            copy.wait_recv()
+        for t in (0, wide - 1):
+            pad[0, t] = below[cols - 1 + t]
+
+    def outer_above():
+        for copy in first_down(False, (-1, 1)):
+            copy.wait_recv()
+        for t in (0, wide - 1):
+            pad[rows + 1, t] = above[cols - 1 + t]
+
+    def whole_below():
+        for copy in first_up(True):
+            copy.wait_recv()
         for t in range(wide):
             pad[0, t] = below[start_below + t] - jump_below
 
-    def fields_above():
-        both_ways(at_top, first_down, received)
+    def whole_above():
+        for copy in first_down(True):
+            copy.wait_recv()
         for t in range(wide):
             pad[rows + 1, t] = above[start_above + t] + jump_above
 
-    def prepare_ghosts(r):
-        p = r + 1 + outward(r)
-        for t in range(wide):
-            prepare(p, t, pad[p, t])
-
+    def fields_far():
+        pl.when(at_top)(whole_above)
+        pl.when(at_bottom)(whole_below)
+        pl.when(jnp.logical_not(jnp.logical_or(at_top, at_bottom)))(inner_below)
+
+    def fields_outer():
+        either(at_top, outer_below, outer_above)
+        pl.when(jnp.logical_not(jnp.logical_or(at_top, at_bottom)))(outer_below)
+
+    def ghost_row(r):
+        return r + 1 + outward(r)
+
+    def inner(r, c):
+        return [(a, b, place) for a, b, place in beyond(r) if 0 <= c + b < cols]
+
+    def outer(r, c):
+        return [(a, b, place) for a, b, place in beyond(r) if not 0 <= c + b < cols]
+
+    def inner_density(r):
+        for t in range(1, wide - 1):
+            prepare(ghost_row(r), t, pad[ghost_row(r), t])
+        for c in range(cols):
+            partial[r, c] = add_pairs(r, c, partial[r, c], inner(r, c))
+
+    with jax.named_scope("recvnear"):
+        either(at_top, inner_below, inner_above)
+    with jax.named_scope("near"):
+        inner_density(near_row)
+    with jax.named_scope("recvfar"):
+        fields_far()
+    with jax.named_scope("far"):
+        inner_density(far_row)
     with jax.named_scope("recvside"):
         for copy in first_sides:
             copy.wait_recv()
-    with jax.named_scope("recvnear"):
-        either(at_top, fields_below, fields_above)
-    with jax.named_scope("near"):
+        fields_outer()
+    with jax.named_scope("side"):
+        for r in (near_row, far_row):
+            for t in (0, wide - 1):
+                prepare(ghost_row(r), t, pad[ghost_row(r), t])
         for r in range(rows):
             prepare(r + 1, 0, left[r])
             prepare(r + 1, cols + 1, right[r])
-        prepare_ghosts(near_row)
-        ghost_density(near_row)
-    either(
-        at_top,
-        lambda: both_ways(at_bottom, second_down, start),
-        lambda: both_ways(at_top, second_up, start),
-    )
-    with jax.named_scope("recvfar"):
-        either(at_top, fields_above, fields_below)
-    with jax.named_scope("far"):
-        prepare_ghosts(far_row)
-        ghost_density(far_row)
-    either(
-        at_top,
-        lambda: both_ways(at_top, second_up, start),
-        lambda: both_ways(at_bottom, second_down, start),
-    )
+        for r in range(rows):
+            for c in (0, cols - 1):
+                partial[r, c] = add_pairs(r, c, partial[r, c], sideways(r, c))
+        for r in (near_row, far_row):
+            for c in (0, cols - 1):
+                partial[r, c] = add_pairs(r, c, partial[r, c], outer(r, c))
+        for r in range(rows):
+            for c in range(cols):
+                finish(r, c, partial[r, c])
+
+    def send_rho(low_first):
+        def send():
+            if low_first:
+                both_ways(at_bottom, second_down, start)
+            both_ways(at_top, second_up, start)
+            if not low_first:
+                both_ways(at_bottom, second_down, start)
+
+        return send
+
     for copy in second_sides:
         copy.start()
+    either(at_bottom, send_rho(True), send_rho(False))
 
     upper_half = row8 >= 4
+
+    def lhs(r, c, a, b):
+        inverse = jnp.broadcast_to(rho_pad[r + 1 + a, c + 1 + b], (8, slots))
+        w = wides[r + 1 + a, c + 1 + b]
+        moment = moments[r + 1 + a, c + 1 + b]
+        rise = jnp.asarray(a, jnp.float32)
+        offset = jnp.where(row8 % 4 == 1, float(b), jnp.where(row8 % 4 == 2, rise, 0.0))
+        moment = moment + offset * w
+        g_rows = split2(jnp.where(upper_half, moment * inverse, moment))
+        k_rows = split2(flows[r + 1 + a, c + 1 + b] * inverse)
+        return jnp.concatenate([g_rows, k_rows], axis=0), k_rows
+
+    def gathered(sums, soft):
+        g_sum = sums[0:8] + sums[8:16]
+        k_sum = (sums[16:24] + sums[24:32]) - SOFT_Q * (soft[0:8] + soft[8:16])
+        return jnp.concatenate([g_sum, k_sum], axis=0)
 
     def push(r, c, pairs):
         i = r * cols + c
-        steps = rows_of(r)
         g_lhs, k_lhs, g_rhs, l_rhs = [], [], [], []
-        for role, b in pairs:
-            a = steps[role]
-            inverse = jnp.broadcast_to(rho_pad[r + 1 + a, c + 1 + b], (8, slots))
-            w = wides[r + 1 + a, c + 1 + b]
-            moment = moments[r + 1 + a, c + 1 + b]
-            rise = jnp.asarray(a, jnp.float32)
-            offset = jnp.where(row8 % 4 == 1, float(b), jnp.where(row8 % 4 == 2, rise, 0.0))
-            moment = moment + offset * w
-            g_rows = split2(jnp.where(upper_half, moment * inverse, moment))
-            k_rows = split2(flows[r + 1 + a, c + 1 + b] * inverse)
-            both = jnp.concatenate([g_rows, k_rows], axis=0)
+        for a, b, place in pairs:
+            both, k_rows = lhs(r, c, a, b)
             g_lhs += [both, both]
             k_lhs.append(k_rows)
-            place = role * 3 + b + 1
             g_rhs.append(g_pairs[i, place])
             l_rhs.append(l_pairs[i, place])
         sums = dot(jnp.concatenate(g_lhs, axis=1), jnp.concatenate(g_rhs, axis=0))
         soft = dot(jnp.concatenate(k_lhs, axis=1), jnp.concatenate(l_rhs, axis=0))
-        g_sum = sums[0:8] + sums[8:16]
-        k_sum = (sums[16:24] + sums[24:32]) - SOFT_Q * (soft[0:8] + soft[8:16])
-        return jnp.concatenate([g_sum, k_sum], axis=0)
+        return gathered(sums, soft)
+
+    def turned_dot(x, y):
+        return lax.dot_general(x, y, (((1,), (1,)), ((), ())), preferred_element_type=jnp.float32)
+
+    def push_back(r, c):
+        g_lhs, k_lhs, g_rhs, l_rhs = [], [], [], []
+        for row, col, a, b, place in back(r, c):
+            both, k_rows = lhs(r, c, a, b)
+            i = row * cols + col
+            g_lhs += [both, both]
+            k_lhs.append(k_rows)
+            g_rhs += [g_pairs[i, place, pl.ds(k * slots, slots)] for k in (0, 1)]
+            l_rhs.append(l_pairs[i, place])
+        sums = turned_dot(jnp.concatenate(g_lhs, axis=1), jnp.concatenate(g_rhs, axis=1))
+        soft = turned_dot(jnp.concatenate(k_lhs, axis=1), jnp.concatenate(l_rhs, axis=1))
+        return gathered(sums, soft)
 
     def settle(r, c, sums):
         f = pad[r + 1, c + 1]
@@ -385,18 +482,13 @@
         for k in range(3):
             acc_ref[r, k, pl.ds(c, 1), :] = accel[k : k + 1]
 
-    def own_force(t, carry):
-        r = t * last
-        for c in range(cols):
-            force_sum[r, c] = push(r, c, edge_pairs(c, inside, False))
-        return carry
-
     with jax.named_scope("ownforce"):
-        lax.fori_loop(0, 2, own_force, 0)
-
-    def ghost_force(r):
-        for c in range(cols):
-            settle(r, c, force_sum[r, c] + push(r, c, edge_pairs(c, beyond, True)))
+        for r in range(rows):
+            for c in range(cols):
+                total = push(r, c, [(a, b, OWN.index((a, b))) for a, b in forward(r, c)])
+                if back(r, c):
+                    total = total + push_back(r, c)
+                force_sum[r, c] = total
 
     def rho_from_below():
         both_ways(at_bottom, second_up, received)
@@ -408,20 +500,28 @@
         for t in range(wide):
             rho_pad[rows + 1, t] = rho_above[start_above + t]
 
+    with jax.named_scope("rhonear"):
+        either(at_top, rho_from_below, rho_from_above)
+    with jax.named_scope("nearforce"):
+        for c in range(cols):
+            force_sum[near_row, c] += push(near_row, c, beyond(near_row))
     with jax.named_scope("rhoside"):
         for copy in second_sides:
             copy.wait_recv()
     for r in range(rows):
         rho_pad[r + 1, 0] = rho_left[r]
         rho_pad[r + 1, cols + 1] = rho_right[r]
-    with jax.named_scope("rhonear"):
-        either(at_top, rho_from_below, rho_from_above)
-    with jax.named_scope("nearforce"):
-        ghost_force(near_row)
     with jax.named_scope("rhofar"):
         either(at_top, rho_from_above, rho_from_below)
     with jax.named_scope("farforce"):
-        ghost_force(far_row)
+        for r in range(rows):
+            for c in (0, cols - 1):
+                force_sum[r, c] += push(r, c, sideways(r, c))
+        for c in range(cols):
+            force_sum[far_row, c] += push(far_row, c, beyond(far_row))
+        for r in range(rows):
+            for c in range(cols):
+                settle(r, c, force_sum[r, c])
     both_ways(at_top, first_up, sent)
     both_ways(at_bottom, first_down, sent)
     both_ways(at_top, second_up, sent)
@@ -477,10 +577,13 @@
             pltpu.VMEM((rows + 2, cols + 2, 8, slots), f32),
             pltpu.VMEM((rows + 2, cols + 2, 8, slots), f32),
             pltpu.VMEM((rows + 2, cols + 2, 8, slots), f32),
+            pltpu.VMEM((rows, cols, 3, 8, slots), f32),
+            pltpu.VMEM((rows, cols, 3, 8, slots), f32),
             pltpu.VMEM((rows, cols, 8, slots), f32),
+            pltpu.VMEM((rows, cols, slots, slots), f32),
             pltpu.VMEM((rows, cols, 16, slots), f32),
-            pltpu.VMEM((cells, 9, 2 * slots, slots), bf16),
-            pltpu.VMEM((cells, 9, slots, slots), bf16),
+            pltpu.VMEM((cells, PLACES, 2 * slots, slots), bf16),
+            pltpu.VMEM((cells, PLACES, slots, slots), bf16),
             dma((8,)),
             dma((8,)),
             dma((8,)),

time: 21.6 us -> 20.2 us (0.935)
  Pallas kernels: 20.2 us -> 18.7 us
    pallas_call x1, Pallas kernels: 19.5 us -> 18.1 us  [local(): pl.pallas_call(functools.partial(kernel, n, m), out_shape=(pltpu.VMEM((ro...]
where the time goes in v3:
time: 20.2 us; the launch traced here: 20 us
  Pallas kernels  18.7 us (93%)
  between operations  1.29 us (6%)
    pallas_call x1, Pallas kernels, local(): pl.pallas_call(functools.partial(kernel, n, m), out_shape=(pltpu.VMEM((ro...  18.1 us
    pallas_call x1, Pallas kernels, local(): pl.pallas_call(relay, out_shape=(jax.ShapeDtypeStruct((rows, cols, slots)...  0.63 us

profile of v3, /device:TPU:0, one launch (start us, length us, event | category | flops | bytes accessed | tf_op | source)
XLA Modules:
  0.0 20.0 jit_solution(17149985439587106085)
XLA Ops:
  1.3 18.1 %shard_map.68 = (f32[2,8,128]{2,1,0:T(8,128)S(1)}, f32[2,3,8,128]{3,2,1,0:T(8,128)S(1)}) custom-call(f32[2,3,8,128]{3,2,1,0:T(8,128)} %bitcast.3, f32[2,3,8,128]{3,2,1,0:T(8,128)} %bitcast.4, f32[2,8,128]{2,1,0:T(8,128)} %mass_hbm.1, s32[2,8]{1,0:T(2,128)} %counts_hbm.1, s32[1]{0:T(128)S(6)} %copy.7.shift_ref), custom_call_target="tpu_custom_call" | custom-call | tf_op jit(solution)/shard_map/pallas_call | solution.py:550
  19.4 0.6 %shard_map.69 = (f32[2,8,128]{2,1,0:T(8,128)}, f32[2,3,8,128]{3,2,1,0:T(8,128)}) custom-call(f32[2,8,128]{2,1,0:T(8,128)S(1)} %get-tuple-element.6.density_ref, f32[2,3,8,128]{3,2,1,0:T(8,128)S(1)} %get-tuple-element.7.accel_ref), custom_call_target="tpu_custom_call" | custom-call | tf_op jit(solution)/shard_map/pallas_call | solution.py:608

commit v4 on v3

--- a/solution.py
+++ b/solution.py
@@ -48,7 +48,7 @@
     own, above, below, left, right, pad,
     rho, rho_above, rho_below, rho_left, rho_right, rho_pad,
     feat, mass_wide, moments, flows, wides, run_rows, rise_rows, partial, backward, force_sum,
-    g_pairs, l_pairs,
+    g_pairs, l_pairs, slope_wait, s_wait,
     send_sem, recv_sem, rho_send_sem, rho_recv_sem, load_sem,
 ):
     rows, _, cols, slots = pos_ref.shape
@@ -143,7 +143,9 @@
     second_sides = to_sides(rho, rho_left, rho_right, rho_send_sem, rho_recv_sem)
 
     last = rows - 1
-    near_row = jnp.where(at_top, 0, last)
+    near_below = jnp.logical_or(at_top, jnp.logical_and(lax.rem(gy, 2) == 1, gy > 0))
+    plain = jnp.logical_not(jnp.logical_or(at_top, at_bottom))
+    near_row = jnp.where(near_below, 0, last)
     far_row = last - near_row
     turn = jnp.where(gx == 0, 2, 0)
 
@@ -175,7 +177,10 @@
         stacked = jnp.concatenate([h, h, mid, h, low, mid], axis=0)
         turned = stacked.T.astype(jnp.bfloat16)
         feat[r, c] = turned
-        mass_wide[r, c] = dot(turned, mass_pick)
+
+    def prepare_force(r, c):
+        f = pad[r, c]
+        w = jnp.broadcast_to(f[6:7], f.shape)
         moment = jnp.where(row8 % 4 == 0, 1.0, f[2:3] - 0.5)
         moment = jnp.where(row8 % 4 == 1, f[0:1] - 0.5, moment)
         moment = jnp.where(row8 % 4 == 2, f[1:2] - 0.5, moment)
@@ -189,6 +194,7 @@
     def prepare_own(r, c):
         f = own[r, c]
         prepare(r + 1, c + 1, f)
+        prepare_force(r + 1, c + 1)
         x = 2.0 * f - 1.0
         for k in (-1, 0, 1):
             run = x[0:1] - 2.0 * k
@@ -224,11 +230,34 @@
     def fold(x):
         return jnp.sum(x.reshape(slots // 8, 8, slots), axis=0)
 
-    def pair(r, c, a, b, place):
+    def keep(i, place, g, s):
+        g_high = g.astype(jnp.bfloat16)
+        g_pairs[i, place, pl.ds(0, slots)] = g_high
+        g_pairs[i, place, pl.ds(slots, slots)] = (
+            g - g_high.astype(jnp.float32)
+        ).astype(jnp.bfloat16)
+        l_pairs[i, place] = g_high / (s + SOFT_Q).astype(jnp.bfloat16)
+
+    def keep_later(r, c, pairs):
         i = r * cols + c
+        for _, _, place in pairs:
+            s = s_wait[i, place - BEYOND]
+            keep(i, place, slope_wait[i, place - BEYOND] * lax.rsqrt(s), s)
+
+    known = set()
+
+    def pair(r, c, a, b, place, name, later=False):
+        i = r * cols + c
+        at = (r + 1 + a, c + 1 + b)
         h, mid, low = split3(rise_rows[r, c, a + 1] + run_rows[r, c, b + 1])
         stacked = jnp.concatenate([h, mid, h, low, h, mid], axis=0).astype(jnp.bfloat16)
-        s = dot(feat[r + 1 + a, c + 1 + b], stacked)
+        if (name, c + b) in known:
+            s, mass = dot(feat[at], stacked), mass_wide[at]
+        else:
+            known.add((name, c + b))
+            both = dot(feat[at], jnp.concatenate([stacked, mass_pick], axis=1))
+            s, mass = both[:, :slots], both[:, slots:]
+            mass_wide[at] = mass
         s = jnp.clip(s, TINY, 4.0)
         inv = lax.rsqrt(s)
         q = s * inv
@@ -236,18 +265,17 @@
         inner = jnp.maximum(outer - q, 0.0)
         inner_sq = inner * inner
         slope = outer * outer - inner_sq
-        g = slope * inv
-        g_high = g.astype(jnp.bfloat16)
-        g_pairs[i, place, pl.ds(0, slots)] = g_high
-        g_pairs[i, place, pl.ds(slots, slots)] = (
-            g - g_high.astype(jnp.float32)
-        ).astype(jnp.bfloat16)
-        l_pairs[i, place] = g_high / (s + SOFT_Q).astype(jnp.bfloat16)
-        return outer * slope + inner_sq
-
-    def add_pairs(r, c, total, pairs):
+        if later:
+            slope_wait[i, place - BEYOND] = slope
+            s_wait[i, place - BEYOND] = s
+        else:
+            keep(i, place, slope * inv, s)
+        return outer * slope + inner_sq, mass
+
+    def add_pairs(r, c, total, pairs, name, later=False):
         for a, b, place in pairs:
-            total = total + fold(pair(r, c, a, b, place) * mass_wide[r + 1 + a, c + 1 + b])
+            value, mass = pair(r, c, a, b, place, r + a if name == "own" else name, later)
+            total = total + fold(value * mass)
         return total
 
     zero8 = jnp.zeros((8, slots), jnp.float32)
@@ -264,8 +292,8 @@
         for c in range(cols):
             total = zero8
             for a, b in forward(r, c):
-                value = pair(r, c, a, b, OWN.index((a, b)))
-                total = total + fold(value * mass_wide[r + 1 + a, c + 1 + b])
+                value, mass = pair(r, c, a, b, OWN.index((a, b)), r + a)
+                total = total + fold(value * mass)
                 if (a, b) != (0, 0):
                     weighed = value.reshape(slots // 8, 8, slots) * wides[r + 1, c + 1][None]
                     weighed = weighed.reshape(slots, slots)
@@ -289,23 +317,22 @@
             own[r, c, pl.ds(6, 1), :] = w
             own[r, c, pl.ds(7, 1), :] = jnp.zeros_like(w)
 
-    def send_fields(low_first):
-        def send():
-            if low_first:
-                both_ways(at_bottom, first_down, start)
-            both_ways(at_top, first_up, start)
-            if not low_first:
-                both_ways(at_bottom, first_down, start)
-
-        return send
-
     def send_stage(stage):
         @pl.when(turn == stage)
         def _():
             pl.semaphore_wait(barrier, len(partners))
             for copy in first_sides:
                 copy.start()
-            either(at_bottom, send_fields(True), send_fields(False))
+            either(
+                near_below,
+                lambda: both_ways(at_top, first_up, start),
+                lambda: both_ways(at_bottom, first_down, start),
+            )
+            either(
+                near_below,
+                lambda: both_ways(at_bottom, first_down, start),
+                lambda: both_ways(at_top, first_up, start),
+            )
 
     with jax.named_scope("send0"):
         send_stage(0)
@@ -356,72 +383,72 @@
         for t in range(wide):
             pad[rows + 1, t] = above[start_above + t] + jump_above
 
-    def fields_far():
+    def plain_below():
+        inner_below()
+        outer_below()
+
+    def plain_above():
+        inner_above()
+        outer_above()
+
+    def ghost_row(r):
+        return r + 1 + outward(r)
+
+    def inner(r, c):
+        return [(a, b, place) for a, b, place in beyond(r) if 0 <= c + b < cols]
+
+    def outer(r, c):
+        return [(a, b, place) for a, b, place in beyond(r) if not 0 <= c + b < cols]
+
+    with jax.named_scope("recvnear"):
+        either(near_below, inner_below, inner_above)
+    with jax.named_scope("near"):
+        for t in range(1, wide - 1):
+            prepare(ghost_row(near_row), t, pad[ghost_row(near_row), t])
+            prepare_force(ghost_row(near_row), t)
+        for c in range(cols):
+            partial[near_row, c] = add_pairs(near_row, c, partial[near_row, c], inner(near_row, c), "near")
+    with jax.named_scope("recvside"):
+        for copy in first_sides:
+            copy.wait_recv()
+        either(near_below, outer_below, outer_above)
+    for r in range(rows):
+        pad[r + 1, 0] = left[r]
+        pad[r + 1, wide - 1] = right[r]
+    with jax.named_scope("recvfar"):
         pl.when(at_top)(whole_above)
         pl.when(at_bottom)(whole_below)
-        pl.when(jnp.logical_not(jnp.logical_or(at_top, at_bottom)))(inner_below)
-
-    def fields_outer():
-        either(at_top, outer_below, outer_above)
-        pl.when(jnp.logical_not(jnp.logical_or(at_top, at_bottom)))(outer_below)
-
-    def ghost_row(r):
-        return r + 1 + outward(r)
-
-    def inner(r, c):
-        return [(a, b, place) for a, b, place in beyond(r) if 0 <= c + b < cols]
-
-    def outer(r, c):
-        return [(a, b, place) for a, b, place in beyond(r) if not 0 <= c + b < cols]
-
-    def inner_density(r):
-        for t in range(1, wide - 1):
-            prepare(ghost_row(r), t, pad[ghost_row(r), t])
-        for c in range(cols):
-            partial[r, c] = add_pairs(r, c, partial[r, c], inner(r, c))
-
-    with jax.named_scope("recvnear"):
-        either(at_top, inner_below, inner_above)
-    with jax.named_scope("near"):
-        inner_density(near_row)
-    with jax.named_scope("recvfar"):
-        fields_far()
+        pl.when(plain)(lambda: either(near_below, plain_above, plain_below))
+    late = [(ghost_row(far_row), t) for t in range(wide)]
+    late += [(ghost_row(near_row), t) for t in (0, wide - 1)]
+    late += [(r + 1, t) for r in range(rows) for t in (0, wide - 1)]
     with jax.named_scope("far"):
-        inner_density(far_row)
-    with jax.named_scope("recvside"):
-        for copy in first_sides:
-            copy.wait_recv()
-        fields_outer()
-    with jax.named_scope("side"):
-        for r in (near_row, far_row):
-            for t in (0, wide - 1):
-                prepare(ghost_row(r), t, pad[ghost_row(r), t])
-        for r in range(rows):
-            prepare(r + 1, 0, left[r])
-            prepare(r + 1, cols + 1, right[r])
+        for r, t in late:
+            prepare(r, t, pad[r, t])
         for r in range(rows):
             for c in (0, cols - 1):
-                partial[r, c] = add_pairs(r, c, partial[r, c], sideways(r, c))
-        for r in (near_row, far_row):
-            for c in (0, cols - 1):
-                partial[r, c] = add_pairs(r, c, partial[r, c], outer(r, c))
-        for r in range(rows):
+                partial[r, c] = add_pairs(r, c, partial[r, c], sideways(r, c), "own", True)
+        for c in (0, cols - 1):
+            partial[near_row, c] = add_pairs(near_row, c, partial[near_row, c], outer(near_row, c), "near", True)
+        for c in range(cols):
+            finish(far_row, c, add_pairs(far_row, c, partial[far_row, c], beyond(far_row), "far", True))
+        for r in range(rows - 1):
+            other = jnp.where(near_row == 0, r, r + 1)
             for c in range(cols):
-                finish(r, c, partial[r, c])
-
-    def send_rho(low_first):
-        def send():
-            if low_first:
-                both_ways(at_bottom, second_down, start)
-            both_ways(at_top, second_up, start)
-            if not low_first:
-                both_ways(at_bottom, second_down, start)
-
-        return send
-
+                finish(other, c, partial[other, c])
+
+    either(
+        near_below,
+        lambda: both_ways(at_top, second_up, start),
+        lambda: both_ways(at_bottom, second_down, start),
+    )
     for copy in second_sides:
         copy.start()
-    either(at_bottom, send_rho(True), send_rho(False))
+    either(
+        near_below,
+        lambda: both_ways(at_bottom, second_down, start),
+        lambda: both_ways(at_top, second_up, start),
+    )
 
     upper_half = row8 >= 4
 
@@ -482,6 +509,16 @@
         for k in range(3):
             acc_ref[r, k, pl.ds(c, 1), :] = accel[k : k + 1]
 
+    with jax.named_scope("later"):
+        for r, t in late:
+            prepare_force(r, t)
+        for r in range(rows):
+            for c in (0, cols - 1):
+                keep_later(r, c, sideways(r, c))
+        for c in (0, cols - 1):
+            keep_later(near_row, c, outer(near_row, c))
+        for c in range(cols):
+            keep_later(far_row, c, beyond(far_row))
     with jax.named_scope("ownforce"):
         for r in range(rows):
             for c in range(cols):
@@ -490,38 +527,76 @@
                     total = total + push_back(r, c)
                 force_sum[r, c] = total
 
-    def rho_from_below():
-        both_ways(at_bottom, second_up, received)
+    def rho_inner_below():
+        second_up(False, (0,))[0].wait_recv()
+        for t in range(1, wide - 1):
+            rho_pad[0, t] = rho_below[cols - 1 + t]
+
+    def rho_inner_above():
+        second_down(False, (0,))[0].wait_recv()
+        for t in range(1, wide - 1):
+            rho_pad[rows + 1, t] = rho_above[cols - 1 + t]
+
+    def rho_outer_below():
+        for copy in second_up(False, (-1, 1)):
+            copy.wait_recv()
+        for t in (0, wide - 1):
+            rho_pad[0, t] = rho_below[cols - 1 + t]
+
+    def rho_outer_above():
+        for copy in second_down(False, (-1, 1)):
+            copy.wait_recv()
+        for t in (0, wide - 1):
+            rho_pad[rows + 1, t] = rho_above[cols - 1 + t]
+
+    def rho_whole_below():
+        for copy in second_up(True):
+            copy.wait_recv()
         for t in range(wide):
             rho_pad[0, t] = rho_below[start_below + t]
 
-    def rho_from_above():
-        both_ways(at_top, second_down, received)
+    def rho_whole_above():
+        for copy in second_down(True):
+            copy.wait_recv()
         for t in range(wide):
             rho_pad[rows + 1, t] = rho_above[start_above + t]
 
+    def rho_plain_below():
+        rho_inner_below()
+        rho_outer_below()
+
+    def rho_plain_above():
+        rho_inner_above()
+        rho_outer_above()
+
     with jax.named_scope("rhonear"):
-        either(at_top, rho_from_below, rho_from_above)
+        either(near_below, rho_inner_below, rho_inner_above)
     with jax.named_scope("nearforce"):
         for c in range(cols):
-            force_sum[near_row, c] += push(near_row, c, beyond(near_row))
+            force_sum[near_row, c] += push(near_row, c, inner(near_row, c))
     with jax.named_scope("rhoside"):
         for copy in second_sides:
             copy.wait_recv()
+        either(near_below, rho_outer_below, rho_outer_above)
     for r in range(rows):
         rho_pad[r + 1, 0] = rho_left[r]
         rho_pad[r + 1, cols + 1] = rho_right[r]
     with jax.named_scope("rhofar"):
-        either(at_top, rho_from_above, rho_from_below)
-    with jax.named_scope("farforce"):
+        pl.when(at_top)(rho_whole_above)
+        pl.when(at_bottom)(rho_whole_below)
+        pl.when(plain)(lambda: either(near_below, rho_plain_above, rho_plain_below))
+    with jax.named_scope("lastforce"):
         for r in range(rows):
             for c in (0, cols - 1):
                 force_sum[r, c] += push(r, c, sideways(r, c))
+        for c in (0, cols - 1):
+            force_sum[near_row, c] += push(near_row, c, outer(near_row, c))
         for c in range(cols):
-            force_sum[far_row, c] += push(far_row, c, beyond(far_row))
-        for r in range(rows):
+            settle(far_row, c, force_sum[far_row, c] + push(far_row, c, beyond(far_row)))
+        for r in range(rows - 1):
+            other = jnp.where(near_row == 0, r, r + 1)
             for c in range(cols):
-                settle(r, c, force_sum[r, c])
+                settle(other, c, force_sum[other, c])
     both_ways(at_top, first_up, sent)
     both_ways(at_bottom, first_down, sent)
     both_ways(at_top, second_up, sent)
@@ -584,6 +659,8 @@
             pltpu.VMEM((rows, cols, 16, slots), f32),
             pltpu.VMEM((cells, PLACES, 2 * slots, slots), bf16),
             pltpu.VMEM((cells, PLACES, slots, slots), bf16),
+            pltpu.VMEM((cells, PLACES - 5, slots, slots), f32),
+            pltpu.VMEM((cells, PLACES - 5, slots, slots), f32),
             dma((8,)),
             dma((8,)),
             dma((8,)),

time: 20.2 us -> 19.4 us (0.960)
  Pallas kernels: 18.7 us -> 18 us
    pallas_call x1, Pallas kernels: 18.1 us -> 17.3 us  [local(): pl.pallas_call(functools.partial(kernel, n, m), out_shape=(pltpu.VMEM((ro...]
where the time goes in v4:
time: 19.4 us; the launch traced here: 19.2 us
  Pallas kernels  18 us (93%)
  between operations  1.29 us (7%)
    pallas_call x1, Pallas kernels, local(): pl.pallas_call(functools.partial(kernel, n, m), out_shape=(pltpu.VMEM((ro...  17.3 us
    pallas_call x1, Pallas kernels, local(): pl.pallas_call(relay, out_shape=(jax.ShapeDtypeStruct((rows, cols, slots)...  0.63 us

profile of v4, /device:TPU:0, one launch (start us, length us, event | category | flops | bytes accessed | tf_op | source)
XLA Modules:
  0.0 19.2 jit_solution(322134599453618762)
XLA Ops:
  1.3 17.3 %shard_map.68 = (f32[2,8,128]{2,1,0:T(8,128)S(1)}, f32[2,3,8,128]{3,2,1,0:T(8,128)S(1)}) custom-call(f32[2,3,8,128]{3,2,1,0:T(8,128)} %bitcast.3, f32[2,3,8,128]{3,2,1,0:T(8,128)} %bitcast.4, f32[2,8,128]{2,1,0:T(8,128)} %mass_hbm.1, s32[2,8]{1,0:T(2,128)} %counts_hbm.1, s32[1]{0:T(128)S(6)} %copy.7.shift_ref), custom_call_target="tpu_custom_call" | custom-call | tf_op jit(solution)/shard_map/pallas_call | solution.py:625
  18.6 0.6 %shard_map.69 = (f32[2,8,128]{2,1,0:T(8,128)}, f32[2,3,8,128]{3,2,1,0:T(8,128)}) custom-call(f32[2,8,128]{2,1,0:T(8,128)S(1)} %get-tuple-element.6.density_ref, f32[2,3,8,128]{3,2,1,0:T(8,128)S(1)} %get-tuple-element.7.accel_ref), custom_call_target="tpu_custom_call" | custom-call | tf_op jit(solution)/shard_map/pallas_call | solution.py:685

commit v5 on v4

--- a/solution.py
+++ b/solution.py
@@ -45,11 +45,12 @@
 def kernel(
     n, m, pos_hbm, vel_hbm, mass_hbm, counts_hbm, shift_ref, dens_ref, acc_ref,
     pos_ref, vel_ref, mass_ref, counts_ref,
-    own, above, below, left, right, pad,
+    own, above, below, left, right,
+    own_v, above_v, below_v, left_v, right_v, pad,
     rho, rho_above, rho_below, rho_left, rho_right, rho_pad,
     feat, mass_wide, moments, flows, wides, run_rows, rise_rows, partial, backward, force_sum,
     g_pairs, l_pairs, slope_wait, s_wait,
-    send_sem, recv_sem, rho_send_sem, rho_recv_sem, load_sem,
+    send_sem, recv_sem, vel_send_sem, vel_recv_sem, rho_recv_sem,
 ):
     rows, _, cols, slots = pos_ref.shape
     gy, gx = lax.axis_index("gy"), lax.axis_index("gx")
@@ -70,7 +71,7 @@
     for device in partners:
         pl.semaphore_signal(barrier, inc=1, device_id=device, device_id_type=MESH)
     loads = [
-        pltpu.make_async_copy(src, dst, load_sem.at[i])
+        pltpu.make_async_copy(src, dst, send_sem.at[i])
         for i, (src, dst) in enumerate([
             (pos_hbm, pos_ref), (vel_hbm, vel_ref), (mass_hbm, mass_ref),
             (counts_hbm, counts_ref),
@@ -138,9 +139,12 @@
     first_up = to_up(own, below, send_sem, recv_sem)
     first_down = to_down(own, above, send_sem, recv_sem)
     first_sides = to_sides(own, left, right, send_sem, recv_sem)
-    second_up = to_up(rho, rho_below, rho_send_sem, rho_recv_sem)
-    second_down = to_down(rho, rho_above, rho_send_sem, rho_recv_sem)
-    second_sides = to_sides(rho, rho_left, rho_right, rho_send_sem, rho_recv_sem)
+    speed_up = to_up(own_v, below_v, vel_send_sem, vel_recv_sem)
+    speed_down = to_down(own_v, above_v, vel_send_sem, vel_recv_sem)
+    speed_sides = to_sides(own_v, left_v, right_v, vel_send_sem, vel_recv_sem)
+    second_up = to_up(rho, rho_below, send_sem, rho_recv_sem)
+    second_down = to_down(rho, rho_above, send_sem, rho_recv_sem)
+    second_sides = to_sides(rho, rho_left, rho_right, send_sem, rho_recv_sem)
 
     last = rows - 1
     near_below = jnp.logical_or(at_top, jnp.logical_and(lax.rem(gy, 2) == 1, gy > 0))
@@ -155,7 +159,7 @@
     start_above = cols - 1 - jnp.where(at_top, lag, 0)
     start_below = cols - 1 + jnp.where(at_bottom, lag, 0)
     row8 = lax.broadcasted_iota(jnp.int32, (8, slots), 0)
-    is_vx = jnp.where(row8 == 3, SHEAR_JUMP, 0.0)
+    is_vx = jnp.where(lax.broadcasted_iota(jnp.int32, (4, slots), 0) == 0, SHEAR_JUMP, 0.0)
     jump_above = jnp.where(at_top, 1.0, 0.0) * is_vx
     jump_below = jnp.where(at_bottom, 1.0, 0.0) * is_vx
 
@@ -165,11 +169,11 @@
     mass_pick = jnp.concatenate([mass_row, none, mass_row, none, mass_row, none], axis=0)
     mass_pick = mass_pick.astype(jnp.bfloat16)
 
-    def prepare(r, c, f):
-        pad[r, c] = f
+    def prepare(r, c):
+        f = pad[r, c]
         x = jnp.where(row8 < 3, 2.0 * f - 1.0, 0.0)
         norm = jnp.sum(x * x, axis=0, keepdims=True)
-        w = jnp.broadcast_to(f[6:7], f.shape)
+        w = jnp.broadcast_to(f[3:4], f.shape)
         p = jnp.where(row8 == 3, norm, x)
         p = jnp.where(row8 == 4, 1.0, p)
         p = jnp.where(row8 == 5, w, p)
@@ -180,20 +184,22 @@
 
     def prepare_force(r, c):
         f = pad[r, c]
-        w = jnp.broadcast_to(f[6:7], f.shape)
+        w = jnp.broadcast_to(f[3:4], f.shape)
         moment = jnp.where(row8 % 4 == 0, 1.0, f[2:3] - 0.5)
         moment = jnp.where(row8 % 4 == 1, f[0:1] - 0.5, moment)
         moment = jnp.where(row8 % 4 == 2, f[1:2] - 0.5, moment)
         moments[r, c] = moment * w
-        flow = jnp.where(row8 == 0, 1.0, f[5:6])
-        flow = jnp.where(row8 == 1, f[3:4], flow)
-        flow = jnp.where(row8 == 2, f[4:5], flow)
+        flow = jnp.where(row8 == 0, 1.0, f[6:7])
+        flow = jnp.where(row8 == 1, f[4:5], flow)
+        flow = jnp.where(row8 == 2, f[5:6], flow)
         flows[r, c] = jnp.where(row8 < 4, flow, 0.0) * w
         wides[r, c] = w
 
     def prepare_own(r, c):
-        f = own[r, c]
-        prepare(r + 1, c + 1, f)
+        pad[r + 1, c + 1, pl.ds(0, 4)] = own[r, c]
+        pad[r + 1, c + 1, pl.ds(4, 4)] = own_v[r, c]
+        f = pad[r + 1, c + 1]
+        prepare(r + 1, c + 1)
         prepare_force(r + 1, c + 1)
         x = 2.0 * f - 1.0
         for k in (-1, 0, 1):
@@ -282,7 +288,7 @@
 
     def finish(r, c, total):
         row = W_SCALE * jnp.sum(total, axis=0, keepdims=True)
-        occupied = pad[r + 1, c + 1, 6:7] > 0.0
+        occupied = pad[r + 1, c + 1, 3:4] > 0.0
         dens_ref[r, pl.ds(c, 1), :] = jnp.where(occupied, row, 0.0)
         inverse = 1.0 / jnp.where(occupied, row, 1.0)
         rho[r, c] = inverse
@@ -312,10 +318,10 @@
         for c in range(cols):
             for k in range(3):
                 own[r, c, pl.ds(k, 1), :] = pos_ref[r, k, pl.ds(c, 1), :]
-                own[r, c, pl.ds(3 + k, 1), :] = vel_ref[r, k, pl.ds(c, 1), :]
+                own_v[r, c, pl.ds(k, 1), :] = vel_ref[r, k, pl.ds(c, 1), :]
             w = jnp.where(lane < counts_ref[r, c], mass_ref[r, pl.ds(c, 1), :], 0.0)
-            own[r, c, pl.ds(6, 1), :] = w
-            own[r, c, pl.ds(7, 1), :] = jnp.zeros_like(w)
+            own[r, c, pl.ds(3, 1), :] = w
+            own_v[r, c, pl.ds(3, 1), :] = jnp.zeros_like(w)
 
     def send_stage(stage):
         @pl.when(turn == stage)
@@ -352,36 +358,36 @@
     def inner_below():
         first_up(False, (0,))[0].wait_recv()
         for t in range(1, wide - 1):
-            pad[0, t] = below[cols - 1 + t]
+            pad[0, t, pl.ds(0, 4)] = below[cols - 1 + t]
 
     def inner_above():
         first_down(False, (0,))[0].wait_recv()
         for t in range(1, wide - 1):
-            pad[rows + 1, t] = above[cols - 1 + t]
+            pad[rows + 1, t, pl.ds(0, 4)] = above[cols - 1 + t]
 
     def outer_below():
         for copy in first_up(False, (-1, 1)):
             copy.wait_recv()
         for t in (0, wide - 1):
-            pad[0, t] = below[cols - 1 + t]
+            pad[0, t, pl.ds(0, 4)] = below[cols - 1 + t]
 
     def outer_above():
         for copy in first_down(False, (-1, 1)):
             copy.wait_recv()
         for t in (0, wide - 1):
-            pad[rows + 1, t] = above[cols - 1 + t]
+            pad[rows + 1, t, pl.ds(0, 4)] = above[cols - 1 + t]
 
     def whole_below():
         for copy in first_up(True):
             copy.wait_recv()
         for t in range(wide):
-            pad[0, t] = below[start_below + t] - jump_below
+            pad[0, t, pl.ds(0, 4)] = below[start_below + t]
 
     def whole_above():
         for copy in first_down(True):
             copy.wait_recv()
         for t in range(wide):
-            pad[rows + 1, t] = above[start_above + t] + jump_above
+            pad[rows + 1, t, pl.ds(0, 4)] = above[start_above + t]
 
     def plain_below():
         inner_below()
@@ -404,32 +410,41 @@
         either(near_below, inner_below, inner_above)
     with jax.named_scope("near"):
         for t in range(1, wide - 1):
-            prepare(ghost_row(near_row), t, pad[ghost_row(near_row), t])
-            prepare_force(ghost_row(near_row), t)
+            prepare(ghost_row(near_row), t)
         for c in range(cols):
             partial[near_row, c] = add_pairs(near_row, c, partial[near_row, c], inner(near_row, c), "near")
+    both_ways(at_top, first_up, sent)
+    both_ways(at_bottom, first_down, sent)
+    for copy in first_sides:
+        copy.wait_send()
+    for copy in speed_sides:
+        copy.start()
+    both_ways(at_top, speed_up, start)
+    both_ways(at_bottom, speed_down, start)
     with jax.named_scope("recvside"):
         for copy in first_sides:
             copy.wait_recv()
         either(near_below, outer_below, outer_above)
     for r in range(rows):
-        pad[r + 1, 0] = left[r]
-        pad[r + 1, wide - 1] = right[r]
-    with jax.named_scope("recvfar"):
-        pl.when(at_top)(whole_above)
-        pl.when(at_bottom)(whole_below)
-        pl.when(plain)(lambda: either(near_below, plain_above, plain_below))
-    late = [(ghost_row(far_row), t) for t in range(wide)]
-    late += [(ghost_row(near_row), t) for t in (0, wide - 1)]
-    late += [(r + 1, t) for r in range(rows) for t in (0, wide - 1)]
-    with jax.named_scope("far"):
-        for r, t in late:
-            prepare(r, t, pad[r, t])
+        pad[r + 1, 0, pl.ds(0, 4)] = left[r]
+        pad[r + 1, wide - 1, pl.ds(0, 4)] = right[r]
+    beside_cells = [(r + 1, t) for r in range(rows) for t in (0, wide - 1)]
+    beside_cells += [(ghost_row(near_row), t) for t in (0, wide - 1)]
+    with jax.named_scope("side"):
+        for r, t in beside_cells:
+            prepare(r, t)
         for r in range(rows):
             for c in (0, cols - 1):
                 partial[r, c] = add_pairs(r, c, partial[r, c], sideways(r, c), "own", True)
         for c in (0, cols - 1):
             partial[near_row, c] = add_pairs(near_row, c, partial[near_row, c], outer(near_row, c), "near", True)
+    with jax.named_scope("recvfar"):
+        pl.when(at_top)(whole_above)
+        pl.when(at_bottom)(whole_below)
+        pl.when(plain)(lambda: either(near_below, plain_above, plain_below))
+    with jax.named_scope("far"):
+        for t in range(wide):
+            prepare(ghost_row(far_row), t)
         for c in range(cols):
             finish(far_row, c, add_pairs(far_row, c, partial[far_row, c], beyond(far_row), "far", True))
         for r in range(rows - 1):
@@ -504,14 +519,12 @@
         plain = here * sums[0:1] - sums[1:4]
         weighed = here * sums[4:5] - sums[5:8]
         pressure = -SOUND_SQ * (mine * plain + weighed)
-        viscous = (2.0 * VISCOSITY) * mine * (f[3:6] * sums[8:9] - sums[9:12])
-        accel = jnp.where(f[6:7] > 0.0, G_SCALE * (pressure + viscous), 0.0)
+        viscous = (2.0 * VISCOSITY) * mine * (f[4:7] * sums[8:9] - sums[9:12])
+        accel = jnp.where(f[3:4] > 0.0, G_SCALE * (pressure + viscous), 0.0)
         for k in range(3):
             acc_ref[r, k, pl.ds(c, 1), :] = accel[k : k + 1]
 
     with jax.named_scope("later"):
-        for r, t in late:
-            prepare_force(r, t)
         for r in range(rows):
             for c in (0, cols - 1):
                 keep_later(r, c, sideways(r, c))
@@ -569,6 +582,28 @@
         rho_inner_above()
         rho_outer_above()
 
+    with jax.named_scope("recvspeed"):
+        both_ways(at_bottom, speed_up, received)
+        both_ways(at_top, speed_down, received)
+        for copy in speed_sides:
+            copy.wait_recv()
+    with jax.named_scope("flows"):
+        for t in range(wide):
+            pad[0, t, pl.ds(4, 4)] = below_v[start_below + t] - jump_below
+            pad[rows + 1, t, pl.ds(4, 4)] = above_v[start_above + t] + jump_above
+        for r in range(rows):
+            pad[r + 1, 0, pl.ds(4, 4)] = left_v[r]
+            pad[r + 1, wide - 1, pl.ds(4, 4)] = right_v[r]
+        for t in range(wide):
+            prepare_force(0, t)
+            prepare_force(rows + 1, t)
+        for r in range(rows):
+            prepare_force(r + 1, 0)
+            prepare_force(r + 1, wide - 1)
+    both_ways(at_top, speed_up, sent)
+    both_ways(at_bottom, speed_down, sent)
+    for copy in speed_sides:
+        copy.wait_send()
     with jax.named_scope("rhonear"):
         either(near_below, rho_inner_below, rho_inner_above)
     with jax.named_scope("nearforce"):
@@ -581,28 +616,27 @@
     for r in range(rows):
         rho_pad[r + 1, 0] = rho_left[r]
         rho_pad[r + 1, cols + 1] = rho_right[r]
-    with jax.named_scope("rhofar"):
-        pl.when(at_top)(rho_whole_above)
-        pl.when(at_bottom)(rho_whole_below)
-        pl.when(plain)(lambda: either(near_below, rho_plain_above, rho_plain_below))
-    with jax.named_scope("lastforce"):
+    with jax.named_scope("sideforce"):
         for r in range(rows):
             for c in (0, cols - 1):
                 force_sum[r, c] += push(r, c, sideways(r, c))
         for c in (0, cols - 1):
             force_sum[near_row, c] += push(near_row, c, outer(near_row, c))
-        for c in range(cols):
-            settle(far_row, c, force_sum[far_row, c] + push(far_row, c, beyond(far_row)))
         for r in range(rows - 1):
             other = jnp.where(near_row == 0, r, r + 1)
             for c in range(cols):
                 settle(other, c, force_sum[other, c])
-    both_ways(at_top, first_up, sent)
-    both_ways(at_bottom, first_down, sent)
     both_ways(at_top, second_up, sent)
     both_ways(at_bottom, second_down, sent)
-    for copy in first_sides + second_sides:
+    for copy in second_sides:
         copy.wait_send()
+    with jax.named_scope("rhofar"):
+        pl.when(at_top)(rho_whole_above)
+        pl.when(at_bottom)(rho_whole_below)
+        pl.when(plain)(lambda: either(near_below, rho_plain_above, rho_plain_below))
+    with jax.named_scope("farforce"):
+        for c in range(cols):
+            settle(far_row, c, force_sum[far_row, c] + push(far_row, c, beyond(far_row)))
 
 
 def relay(density_ref, accel_ref, density_out, accel_out, sem):
@@ -635,11 +669,16 @@
             pltpu.VMEM((rows, 3, cols, slots), f32),
             pltpu.VMEM((rows, cols, slots), f32),
             pltpu.SMEM((rows, cols), jnp.int32),
-            pltpu.VMEM((rows, cols, 8, slots), f32),
-            pltpu.VMEM((3 * cols, 8, slots), f32),
-            pltpu.VMEM((3 * cols, 8, slots), f32),
-            pltpu.VMEM((rows, 8, slots), f32),
-            pltpu.VMEM((rows, 8, slots), f32),
+            pltpu.VMEM((rows, cols, 4, slots), f32),
+            pltpu.VMEM((3 * cols, 4, slots), f32),
+            pltpu.VMEM((3 * cols, 4, slots), f32),
+            pltpu.VMEM((rows, 4, slots), f32),
+            pltpu.VMEM((rows, 4, slots), f32),
+            pltpu.VMEM((rows, cols, 4, slots), f32),
+            pltpu.VMEM((3 * cols, 4, slots), f32),
+            pltpu.VMEM((3 * cols, 4, slots), f32),
+            pltpu.VMEM((rows, 4, slots), f32),
+            pltpu.VMEM((rows, 4, slots), f32),
             pltpu.VMEM((rows + 2, cols + 2, 8, slots), f32),
             pltpu.VMEM((rows, cols, 1, slots), f32),
             pltpu.VMEM((3 * cols, 1, slots), f32),
@@ -665,7 +704,7 @@
             dma((8,)),
             dma((8,)),
             dma((8,)),
-            dma((4,)),
+            dma((8,)),
         ],
         compiler_params=pltpu.CompilerParams(
             collective_id=0, has_side_effects=True, vmem_limit_bytes=VMEM_LIMIT

time: 19.4 us -> 18.7 us (0.964)
  Pallas kernels: 18 us -> 17.3 us
    pallas_call x1, Pallas kernels: 17.3 us -> 16.6 us  [local(): pl.pallas_call(functools.partial(kernel, n, m), out_shape=(pltpu.VMEM((ro...]
where the time goes in v5:
time: 18.7 us; the launch traced here: 18.5 us
  Pallas kernels  17.3 us (93%)
  between operations  1.29 us (7%)
    pallas_call x1, Pallas kernels, local(): pl.pallas_call(functools.partial(kernel, n, m), out_shape=(pltpu.VMEM((ro...  16.6 us
    pallas_call x1, Pallas kernels, local(): pl.pallas_call(relay, out_shape=(jax.ShapeDtypeStruct((rows, cols, slots)...  0.63 us

profile of v5, /device:TPU:0, one launch (start us, length us, event | category | flops | bytes accessed | tf_op | source)
XLA Modules:
  0.0 18.5 jit_solution(1146916845242456321)
XLA Ops:
  1.3 16.6 %shard_map.68 = (f32[2,8,128]{2,1,0:T(8,128)S(1)}, f32[2,3,8,128]{3,2,1,0:T(8,128)S(1)}) custom-call(f32[2,3,8,128]{3,2,1,0:T(8,128)} %bitcast.3, f32[2,3,8,128]{3,2,1,0:T(8,128)} %bitcast.4, f32[2,8,128]{2,1,0:T(8,128)} %mass_hbm.1, s32[2,8]{1,0:T(2,128)} %counts_hbm.1, s32[1]{0:T(128)S(6)} %copy.7.shift_ref), custom_call_target="tpu_custom_call" | custom-call | tf_op jit(solution)/shard_map/pallas_call | solution.py:659
  17.9 0.6 %shard_map.69 = (f32[2,8,128]{2,1,0:T(8,128)}, f32[2,3,8,128]{3,2,1,0:T(8,128)}) custom-call(f32[2,8,128]{2,1,0:T(8,128)S(1)} %get-tuple-element.6.density_ref, f32[2,3,8,128]{3,2,1,0:T(8,128)S(1)} %get-tuple-element.7.accel_ref), custom_call_target="tpu_custom_call" | custom-call | tf_op jit(solution)/shard_map/pallas_call | solution.py:724

commit v6 on v5

--- a/solution.py
+++ b/solution.py
@@ -257,10 +257,11 @@
         at = (r + 1 + a, c + 1 + b)
         h, mid, low = split3(rise_rows[r, c, a + 1] + run_rows[r, c, b + 1])
         stacked = jnp.concatenate([h, mid, h, low, h, mid], axis=0).astype(jnp.bfloat16)
-        if (name, c + b) in known:
+        key = name if isinstance(name, tuple) else (name, c + b)
+        if key in known:
             s, mass = dot(feat[at], stacked), mass_wide[at]
         else:
-            known.add((name, c + b))
+            known.add(key)
             both = dot(feat[at], jnp.concatenate([stacked, mass_pick], axis=1))
             s, mass = both[:, :slots], both[:, slots:]
             mass_wide[at] = mass
@@ -438,25 +439,43 @@
                 partial[r, c] = add_pairs(r, c, partial[r, c], sideways(r, c), "own", True)
         for c in (0, cols - 1):
             partial[near_row, c] = add_pairs(near_row, c, partial[near_row, c], outer(near_row, c), "near", True)
+        for r in range(rows - 1):
+            other = jnp.where(near_row == 0, r, r + 1)
+            for c in range(cols):
+                finish(other, c, partial[other, c])
     with jax.named_scope("recvfar"):
         pl.when(at_top)(whole_above)
         pl.when(at_bottom)(whole_below)
         pl.when(plain)(lambda: either(near_below, plain_above, plain_below))
+    leftward = gx < n // 2
+    turned = jnp.where(leftward, -1, 1)
+    first_column = jnp.where(leftward, cols - 1, 0)
+
+    def far_cells(places):
+        for u in places:
+            c = first_column + turned * u
+            total = partial[far_row, c]
+            for d in (-1, 0, 1):
+                b = turned * d
+                value, mass = pair(
+                    far_row, c, outward(far_row), b, BEYOND + b + 1, ("far", u + d), True
+                )
+                total = total + fold(value * mass)
+            finish(far_row, c, total)
+
+    def far_send(ks):
+        either(
+            near_below,
+            lambda: both_ways(at_top, lambda full: second_up(full, ks), start),
+            lambda: both_ways(at_bottom, lambda full: second_down(full, ks), start),
+        )
+
+    urgent = sorted({*range(reach + 1), cols - 1})
     with jax.named_scope("far"):
-        for t in range(wide):
-            prepare(ghost_row(far_row), t)
-        for c in range(cols):
-            finish(far_row, c, add_pairs(far_row, c, partial[far_row, c], beyond(far_row), "far", True))
-        for r in range(rows - 1):
-            other = jnp.where(near_row == 0, r, r + 1)
-            for c in range(cols):
-                finish(other, c, partial[other, c])
-
-    either(
-        near_below,
-        lambda: both_ways(at_top, second_up, start),
-        lambda: both_ways(at_bottom, second_down, start),
-    )
+        for v in range(wide):
+            prepare(ghost_row(far_row), first_column + 1 + turned * (v - 1))
+        far_cells(urgent)
+    either(leftward, lambda: far_send((-1,)), lambda: far_send((1,)))
     for copy in second_sides:
         copy.start()
     either(
@@ -464,6 +483,9 @@
         lambda: both_ways(at_bottom, second_down, start),
         lambda: both_ways(at_top, second_up, start),
     )
+    with jax.named_scope("far2"):
+        far_cells([u for u in range(cols) if u not in urgent])
+    either(leftward, lambda: far_send((0, 1)), lambda: far_send((0, -1)))
 
     upper_half = row8 >= 4
 

time: 18.7 us -> 18.6 us (level)
  Pallas kernels: 17.3 us -> 17.1 us
where the time goes in v6:
time: 18.6 us; the launch traced here: 18.4 us
  Pallas kernels  17.1 us (92%)
  between operations  1.29 us (7%)
    pallas_call x1, Pallas kernels, local(): pl.pallas_call(functools.partial(kernel, n, m), out_shape=(pltpu.VMEM((ro...  16.5 us
    pallas_call x1, Pallas kernels, local(): pl.pallas_call(relay, out_shape=(jax.ShapeDtypeStruct((rows, cols, slots)...  0.63 us

profile of v6, /device:TPU:0, one launch (start us, length us, event | category | flops | bytes accessed | tf_op | source)
XLA Modules:
  0.0 18.4 jit_solution(2912181112491272356)
XLA Ops:
  1.3 16.5 %shard_map.68 = (f32[2,8,128]{2,1,0:T(8,128)S(1)}, f32[2,3,8,128]{3,2,1,0:T(8,128)S(1)}) custom-call(f32[2,3,8,128]{3,2,1,0:T(8,128)} %bitcast.3, f32[2,3,8,128]{3,2,1,0:T(8,128)} %bitcast.4, f32[2,8,128]{2,1,0:T(8,128)} %mass_hbm.1, s32[2,8]{1,0:T(2,128)} %counts_hbm.1, s32[1]{0:T(128)S(6)} %copy.7.shift_ref), custom_call_target="tpu_custom_call" | custom-call | tf_op jit(solution)/shard_map/pallas_call | solution.py:681
  17.8 0.6 %shard_map.69 = (f32[2,8,128]{2,1,0:T(8,128)}, f32[2,3,8,128]{3,2,1,0:T(8,128)}) custom-call(f32[2,8,128]{2,1,0:T(8,128)S(1)} %get-tuple-element.6.density_ref, f32[2,3,8,128]{3,2,1,0:T(8,128)S(1)} %get-tuple-element.7.accel_ref), custom_call_target="tpu_custom_call" | custom-call | tf_op jit(solution)/shard_map/pallas_call | solution.py:746

commit v7 on v6

--- a/solution.py
+++ b/solution.py
@@ -151,7 +151,7 @@
     plain = jnp.logical_not(jnp.logical_or(at_top, at_bottom))
     near_row = jnp.where(near_below, 0, last)
     far_row = last - near_row
-    turn = jnp.where(gx == 0, 2, 0)
+    turn = jnp.where(gx == 0, 2, jnp.where(gx + gy == 1, 1, 0))
 
     shift = shift_ref[0]
     total_half = half * cols

time: 18.6 us -> 18.6 us (level)
  no operation moved by 1% of the time
where the time goes in v7:
time: 18.6 us; the launch traced here: 18.4 us
  Pallas kernels  17.1 us (92%)
  between operations  1.29 us (7%)
    pallas_call x1, Pallas kernels, local(): pl.pallas_call(functools.partial(kernel, n, m), out_shape=(pltpu.VMEM((ro...  16.5 us
    pallas_call x1, Pallas kernels, local(): pl.pallas_call(relay, out_shape=(jax.ShapeDtypeStruct((rows, cols, slots)...  0.63 us

profile of v7, /device:TPU:0, one launch (start us, length us, event | category | flops | bytes accessed | tf_op | source)
XLA Modules:
  0.0 18.4 jit_solution(2843176146055881498)
XLA Ops:
  1.3 16.5 %shard_map.68 = (f32[2,8,128]{2,1,0:T(8,128)S(1)}, f32[2,3,8,128]{3,2,1,0:T(8,128)S(1)}) custom-call(f32[2,3,8,128]{3,2,1,0:T(8,128)} %bitcast.3, f32[2,3,8,128]{3,2,1,0:T(8,128)} %bitcast.4, f32[2,8,128]{2,1,0:T(8,128)} %mass_hbm.1, s32[2,8]{1,0:T(2,128)} %counts_hbm.1, s32[1]{0:T(128)S(6)} %copy.7.shift_ref), custom_call_target="tpu_custom_call" | custom-call | tf_op jit(solution)/shard_map/pallas_call | solution.py:681
  17.8 0.6 %shard_map.69 = (f32[2,8,128]{2,1,0:T(8,128)}, f32[2,3,8,128]{3,2,1,0:T(8,128)}) custom-call(f32[2,8,128]{2,1,0:T(8,128)S(1)} %get-tuple-element.6.density_ref, f32[2,3,8,128]{3,2,1,0:T(8,128)S(1)} %get-tuple-element.7.accel_ref), custom_call_target="tpu_custom_call" | custom-call | tf_op jit(solution)/shard_map/pallas_call | solution.py:746
